TPU v7x, 32 devices: a whole 2x2x4 slice. The times are simulated.
32 devices in a mesh: section: 8 (over y, x, core), tensor: 4 (over z).
Axes of the slice: x: 2, y: 2, z: 4, core: 2. Of those that a mesh axis runs over, the one named last changes fastest.
Arguments:
- matching: int32 [8], replicated, may hold values from 0 to 7, each once
- lengths: int32 [32], replicated, may hold values from 2 to 255
- queries: bfloat16 [8, 32, 8192], P('section', None, 'tensor'), may hold values from -200 to 200
- kv_cache: bfloat16 [8, 32, 256, 2048], P('section', None, None, 'tensor'), may hold values from -6 to 6
- incoming_key_value: bfloat16 [8, 32, 2048], P('section', None, 'tensor'), may hold values from -6 to 6
- residual: bfloat16 [8, 32, 8192], P('section', None, 'tensor'), may hold values from -6 to 6
- out_weight: bfloat16 [8, 8192, 8192], P('section', 'tensor'), may hold values from -0.09375 to 0.09375
- norm_gain: bfloat16 [8, 8192], P('section', 'tensor'), may hold values from 0.5 to 1.5
Outputs:
- cache_out: bfloat16 [8, 32, 256, 2048], P('section', None, None, 'tensor')
- stream_out: bfloat16 [8, 32, 8192], P('section', None, 'tensor')
- normed_out: bfloat16 [8, 32, 8192], P('section', None, 'tensor')
All inputs are finite; a program needn't handle non-finite values.
Results may differ from a plain program's by a relative error of at most 0.0042.
Values may be sent and summed in bfloat16 or wider, within the bound.
No kernel may reach another device: no remote copies, remote signals or barrier semaphores. Data moves between devices by JAX's collectives and lax.ppermute only.
A program may use at most 128 MiB of HBM per device.

v0:
```python
import math

import jax
import jax.numpy as jnp
from jax import lax
from jax.sharding import PartitionSpec as P

D = 8192
HEAD_SIZE = 128


def fold_rows(member, groups):
    return member.reshape((groups, member.shape[1] // groups) + member.shape[2:])


def attend(lengths, query_vectors, cache_rows, fresh_rows):
    seq_rows, ctx_len, kv_width = cache_rows.shape
    kv_heads = kv_width // (2 * HEAD_SIZE)
    places = lax.broadcasted_iota(jnp.int32, (seq_rows, ctx_len), 1)
    written = places == lengths[:, None]
    updated_cache = jnp.where(written[:, :, None], fresh_rows[:, None, :], cache_rows)
    heads_separated = updated_cache.reshape(seq_rows, ctx_len, kv_heads, 2, HEAD_SIZE)
    key_rows = heads_separated[:, :, :, 0]
    value_rows = heads_separated[:, :, :, 1]
    grouped_queries = query_vectors.reshape(seq_rows, kv_heads, -1, HEAD_SIZE)
    scores = jnp.einsum(
        "bgrd,bsgd->bgrs", grouped_queries, key_rows, preferred_element_type=jnp.float32
    ) / math.sqrt(HEAD_SIZE)
    visible = places <= lengths[:, None]
    scores = jnp.where(visible[:, None, None, :], scores, -1e30)
    weights = jax.nn.softmax(scores, axis=-1).astype(jnp.bfloat16)
    attended = jnp.einsum(
        "bgrs,bsgd->bgrd", weights, value_rows, preferred_element_type=jnp.float32
    )
    return (updated_cache, attended.astype(jnp.bfloat16).reshape(seq_rows, -1))


def decode_layer(lengths, queries, kv_cache, incoming_key_value, residual, out_weight, norm_gain):
    updated_cache, attended = attend(lengths, queries[0], kv_cache[0], incoming_key_value[0])
    partial_value = jnp.dot(attended, out_weight[0], preferred_element_type=jnp.float32)
    own_res = residual[0].astype(jnp.float32)
    stream = own_res + lax.psum_scatter(partial_value, "tensor", scatter_dimension=1, tiled=True)
    squares = lax.psum(jnp.sum(stream * stream, axis=-1, keepdims=True), "tensor")
    normed = stream * lax.rsqrt(squares / D + 1e-05) * norm_gain[0].astype(jnp.float32)
    return (
        updated_cache[None],
        stream.astype(jnp.bfloat16)[None],
        normed.astype(jnp.bfloat16)[None],
    )


def move_results(matching, updated_cache, stream, normed):
    groups = lax.axis_size("section")
    spread = (
        lax.all_to_all(
            fold_rows(updated_cache, groups), "section", split_axis=0, concat_axis=0, tiled=True
        ),
        lax.all_to_all(
            fold_rows(stream, groups), "section", split_axis=0, concat_axis=0, tiled=True
        ),
        lax.all_to_all(
            fold_rows(normed, groups), "section", split_axis=0, concat_axis=0, tiled=True
        ),
    )
    landed = (
        lax.all_to_all(
            jnp.take(spread[0], matching, axis=0),
            "section",
            split_axis=0,
            concat_axis=0,
            tiled=True,
        ),
        lax.all_to_all(
            jnp.take(spread[1], matching, axis=0),
            "section",
            split_axis=0,
            concat_axis=0,
            tiled=True,
        ),
        lax.all_to_all(
            jnp.take(spread[2], matching, axis=0),
            "section",
            split_axis=0,
            concat_axis=0,
            tiled=True,
        ),
    )
    return (
        landed[0].reshape(updated_cache.shape),
        landed[1].reshape(stream.shape),
        landed[2].reshape(normed.shape),
    )


def on_device(
    matching, lengths, queries, kv_cache, incoming_key_value, residual, out_weight, norm_gain
):
    updated_cache, stream, normed = decode_layer(
        lengths, queries, kv_cache, incoming_key_value, residual, out_weight, norm_gain
    )
    updated_cache, stream, normed = move_results(matching, updated_cache, stream, normed)
    return (updated_cache, stream, normed)


def solution(mesh):
    return jax.shard_map(
        on_device,
        mesh=mesh,
        in_specs=(
            P(),
            P(),
            P("section", None, "tensor"),
            P("section", None, None, "tensor"),
            P("section", None, "tensor"),
            P("section", None, "tensor"),
            P("section", "tensor", None),
            P("section", "tensor"),
        ),
        out_specs=(
            P("section", None, None, "tensor"),
            P("section", None, "tensor"),
            P("section", None, "tensor"),
        ),
        check_vma=False,
    )
```

profile of v0, /device:TPU:0, one launch (start us, length us, event | category | flops | bytes accessed | tf_op | source)
XLA Modules:
  0.0 358.9 jit_solution(12885923463417090091)
XLA Ops:
  8.0 11.9 %copy.13 = bf16[1,32,256,512]{2,3,1,0:T(8,128)(2,1)} copy(bf16[1,32,256,512]{3,2,1,0:T(8,128)(2,1)} %param.13) | data formatting | bytes 16777216 | tf_op args[3]
  19.9 12.0 %copy.14 = bf16[32,256,2,2,128]{4,1,2,0,3:T(8,128)(2,1)} copy(bf16[32,256,2,2,128]{1,4,3,2,0:T(8,128)(2,1)} %bitcast.50) | data formatting | bytes 16777216 | tf_op jit(solution)/shard_map/squeeze | solution.py:39
  32.0 7.5 %broadcast_select_fusion.1 = bf16[32,256,2,2,128]{4,1,2,0,3:T(8,128)(2,1)} fusion(bf16[32,256,2,2,128]{4,1,2,0,3:T(8,128)(2,1)} %copy.14, pred[32,256]{1,0:T(8,128)(4,1)S(1)} %get-tuple-element.9, bf16[32,2,2,128]{3,1,0,2:T(2,128)(2,1)S(1)} %copy.12), kind=kLoop, calls=%fused_computation.7 | loop fusion | flops 4194304 | bytes 16818176 | tf_op jit(solution)/shard_map/jit(_where)/select_n | solution.py:21
  39.5 3.6 fusion.15
  43.0 2.9 fusion.10
  46.0 14.6 %fusion.1 = f32[32,8192]{1,0:T(8,128)} fusion(bf16[1,2048,8192]{2,1,0:T(8,128)(2,1)} %param.16, bf16[4,8,16,128]{3,2,1,0:T(8,128)(2,1)S(1)} %bitcast.51), kind=kOutput, calls=%fused_computation.4 | convolution fusion | flops 1073741824 | bytes 34734080 | tf_op jit(solution)/shard_map/dot_general | solution.py:40
  60.7 30.0 %reduce-scatter.2.cloned.1.call-done = f32[32,2048]{1,0:T(8,128)} async-done(((f32[32,8192]{1,0:T(8,128)}), f32[32,2048]{1,0:T(8,128)}) %reduce-scatter.2.cloned.1.call-update) | async-done | bytes 262160 | tf_op jit(solution)/shard_map/reduce_scatter | solution.py:42
  90.7 1.1 multiply_reduce_fusion
  91.8 9.3 %psum.7 = f32[32,1]{0,1:T(1,128)S(1)} all-reduce(f32[32,1]{0,1:T(1,128)S(1)} %bitcast.55), channel_id=1, replica_groups=mesh['section'=8,'tensor'=4] {'tensor'}, use_global_device_ids=true, to_apply=%region_4.6 | all-reduce | flops 32 | bytes 256 | tf_op jit(solution)/shard_map/psum | solution.py:43
  101.1 1.0 multiply_convert_fusion
  102.9 3.7 %all-to-all-start.2 = ((bf16[8,4,2048]{2,1,0:T(4,128)(2,1)}), bf16[8,4,2048]{2,1,0:T(4,128)(2,1)S(1)}, u32[]{:S(2)}, u32[]{:S(2)}) async-start(bf16[8,4,2048]{2,1,0:T(4,128)(2,1)} %reshape_broadcast_in_dim.7), calls=%async_computation.3 | async-start | bytes 262144 | tf_op jit(solution)/shard_map/all_to_all | solution.py:58
  107.3 4.7 %all-to-all-done.2 = bf16[8,4,2048]{2,1,0:T(4,128)(2,1)S(1)} async-done(((bf16[8,4,2048]{2,1,0:T(4,128)(2,1)}), bf16[8,4,2048]{2,1,0:T(4,128)(2,1)S(1)}, u32[]{:S(2)}, u32[]{:S(2)}) %all-to-all-start.2) | async-done | bytes 131104 | tf_op jit(solution)/shard_map/all_to_all | solution.py:58
  112.0 3.4 all-to-all-start.4
  115.4 7.5 %broadcast_select_fusion.2 = bf16[8,4,256,512]{3,2,1,0:T(8,128)(2,1)} fusion(bf16[8,4,256,512]{3,2,1,0:T(8,128)(2,1)} %bitcast.49, pred[8,4,256]{2,1,0:T(4,128)(4,1)S(1)} %iota_compare_fusion.2, bf16[8,4,512]{2,1,0:T(4,128)(2,1)S(1)} %broadcast_in_dim.69), kind=kLoop, calls=%fused_computation.8 | loop fusion | flops 4194304 | bytes 16818176 | tf_op jit(solution)/shard_map/jit(_where)/select_n | solution.py:21
  122.9 5.1 %all-to-all-start = ((bf16[8,4,256,512]{3,2,1,0:T(8,128)(2,1)}), bf16[8,4,256,512]{3,2,1,0:T(8,128)(2,1)}, u32[]{:S(2)}, u32[]{:S(2)}) async-start(bf16[8,4,256,512]{3,2,1,0:T(8,128)(2,1)} %broadcast_select_fusion.2), calls=%async_computation | async-start | bytes 16777216 | tf_op jit(solution)/shard_map/all_to_all | solution.py:55
  129.4 0.9 broadcast_select_fusion.3
  130.2 91.8 %all-to-all-done = bf16[8,4,256,512]{3,2,1,0:T(8,128)(2,1)} async-done(((bf16[8,4,256,512]{3,2,1,0:T(8,128)(2,1)}), bf16[8,4,256,512]{3,2,1,0:T(8,128)(2,1)}, u32[]{:S(2)}, u32[]{:S(2)}) %all-to-all-start) | async-done | bytes 8388640 | tf_op jit(solution)/shard_map/all_to_all | solution.py:55
  222.0 3.4 all-to-all-start.3
  225.4 8.2 %gather_fusion = bf16[8,4,256,512]{3,2,1,0:T(8,128)(2,1)} fusion(bf16[8,4,256,512]{3,2,1,0:T(8,128)(2,1)} %all-to-all-done, s32[1024]{0:T(1024)S(1)} %pad_clamp_fusion), kind=kCustom, calls=%fused_computation.2 | custom fusion | bytes 16777248 | tf_op jit(solution)/shard_map/jit(_take)/gather | solution.py:67
  233.6 4.1 %all-to-all-start.5 = ((bf16[8,4,2048]{2,1,0:T(4,128)(2,1)}), bf16[8,4,2048]{2,1,0:T(4,128)(2,1)S(1)}, u32[]{:S(2)}, u32[]{:S(2)}) async-start(bf16[8,4,2048]{2,1,0:T(4,128)(2,1)} %get-tuple-element.6), calls=%async_computation.6 | async-start | bytes 262144 | tf_op jit(solution)/shard_map/all_to_all | solution.py:80
  237.8 7.6 %broadcast_select_fusion = bf16[8,4,256,512]{3,2,1,0:T(8,128)(2,1)} fusion(bf16[8,4,256,512]{3,2,1,0:T(8,128)(2,1)} %gather_fusion, pred[8]{0:T(512)(128)(4,1)S(1)} %compare_and_fusion), kind=kLoop, calls=%fused_computation.6 | loop fusion | flops 4194304 | bytes 16777224 | tf_op jit(solution)/shard_map/jit(_take)/select_n | solution.py:67
  245.4 5.0 %all-to-all-start.1 = ((bf16[8,4,256,512]{3,2,1,0:T(8,128)(2,1)}), bf16[8,4,256,512]{3,2,1,0:T(8,128)(2,1)}, u32[]{:S(2)}, u32[]{:S(2)}) async-start(bf16[8,4,256,512]{3,2,1,0:T(8,128)(2,1)} %broadcast_select_fusion), calls=%async_computation.1 | async-start | bytes 16777216 | tf_op jit(solution)/shard_map/all_to_all | solution.py:66
  251.7 92.7 %all-to-all-done.1 = bf16[8,4,256,512]{3,2,1,0:T(8,128)(2,1)} async-done(((bf16[8,4,256,512]{3,2,1,0:T(8,128)(2,1)}), bf16[8,4,256,512]{3,2,1,0:T(8,128)(2,1)}, u32[]{:S(2)}, u32[]{:S(2)}) %all-to-all-start.1) | async-done | bytes 8388640 | tf_op jit(solution)/shard_map/all_to_all | solution.py:66
  344.4 7.7 %copy.22 = bf16[1,32,256,512]{3,2,1,0:T(8,128)(2,1)} copy(bf16[1,32,256,512]{3,2,1,0:T(8,128)(2,1)} %bitcast.1) | data formatting | bytes 16777216
  (35 shorter events, 5.2 us)
Async XLA Ops:
  7.2 83.6 %reduce-scatter.2.cloned.1.call-start = ((), (), s32[]{:S(2)}) async-start(), calls=%async_computation.7 | async-start | bytes 1310720 | tf_op jit(solution)/shard_map/reduce_scatter | solution.py:42
  19.9 12.0 %copy-start.2 = (bf16[1,32,512]{2,1,0:T(8,128)(2,1)S(1)}, bf16[1,32,512]{2,1,0:T(8,128)(2,1)}, u32[]{:S(2)}) copy-start(bf16[1,32,512]{2,1,0:T(8,128)(2,1)} %param.14) | copy-start | bytes 98308
  19.9 12.1 %copy-start.1 = (bf16[1,32,2048]{2,1,0:T(8,128)(2,1)S(1)}, bf16[1,32,2048]{2,1,0:T(8,128)(2,1)}, u32[]{:S(2)}) copy-start(bf16[1,32,2048]{2,1,0:T(8,128)(2,1)} %param.12) | copy-start | bytes 393220
  45.9 14.7 %copy-start.4 = (s32[32]{0:T(128)S(1)}, s32[32]{0:T(128)}, u32[]{:S(2)}) copy-start(s32[32]{0:T(128)} %param.11) | copy-start | bytes 388
  45.9 14.7 %copy-start.3 = (bf16[1,2048]{1,0:T(2,128)(2,1)S(1)}, bf16[1,2048]{1,0:T(2,128)(2,1)}, u32[]{:S(2)}) copy-start(bf16[1,2048]{1,0:T(2,128)(2,1)} %param.17) | copy-start | bytes 12292
  46.0 44.8 %copy-start = (bf16[1,32,2048]{2,1,0:T(8,128)(2,1)S(1)}, bf16[1,32,2048]{2,1,0:T(8,128)(2,1)}, u32[]{:S(2)}) copy-start(bf16[1,32,2048]{2,1,0:T(8,128)(2,1)} %param.15) | copy-start | bytes 393220
  102.9 9.2 %all-to-all-start.2 = ((bf16[8,4,2048]{2,1,0:T(4,128)(2,1)}), bf16[8,4,2048]{2,1,0:T(4,128)(2,1)S(1)}, u32[]{:S(2)}, u32[]{:S(2)}) async-start(bf16[8,4,2048]{2,1,0:T(4,128)(2,1)} %reshape_broadcast_in_dim.7), calls=%async_computation.3 | async-start | bytes 262144 | tf_op jit(solution)/shard_map/all_to_all | solution.py:58
  112.0 10.9 %all-to-all-start.4 = ((bf16[8,4,2048]{2,1,0:T(4,128)(2,1)}), bf16[8,4,2048]{2,1,0:T(4,128)(2,1)S(1)}, u32[]{:S(2)}, u32[]{:S(2)}) async-start(bf16[8,4,2048]{2,1,0:T(4,128)(2,1)} %reshape_broadcast_in_dim.8), calls=%async_computation.5 | async-start | bytes 262144 | tf_op jit(solution)/shard_map/all_to_all | solution.py:61
  122.9 5.1 %copy-start.5 = (s32[8]{0:T(128)S(1)}, s32[8]{0:T(128)}, u32[]{:S(2)}) copy-start(s32[8]{0:T(128)} %param.10) | copy-start | bytes 100
  122.9 99.1 %all-to-all-start = ((bf16[8,4,256,512]{3,2,1,0:T(8,128)(2,1)}), bf16[8,4,256,512]{3,2,1,0:T(8,128)(2,1)}, u32[]{:S(2)}, u32[]{:S(2)}) async-start(bf16[8,4,256,512]{3,2,1,0:T(8,128)(2,1)} %broadcast_select_fusion.2), calls=%async_computation | async-start | bytes 16777216 | tf_op jit(solution)/shard_map/all_to_all | solution.py:55
  222.0 11.6 %all-to-all-start.3 = ((bf16[8,4,2048]{2,1,0:T(4,128)(2,1)}), bf16[8,4,2048]{2,1,0:T(4,128)(2,1)S(1)}, u32[]{:S(2)}, u32[]{:S(2)}) async-start(bf16[8,4,2048]{2,1,0:T(4,128)(2,1)} %get-tuple-element.7), calls=%async_computation.4 | async-start | bytes 262144 | tf_op jit(solution)/shard_map/all_to_all | solution.py:73
  233.6 11.8 %all-to-all-start.5 = ((bf16[8,4,2048]{2,1,0:T(4,128)(2,1)}), bf16[8,4,2048]{2,1,0:T(4,128)(2,1)S(1)}, u32[]{:S(2)}, u32[]{:S(2)}) async-start(bf16[8,4,2048]{2,1,0:T(4,128)(2,1)} %get-tuple-element.6), calls=%async_computation.6 | async-start | bytes 262144 | tf_op jit(solution)/shard_map/all_to_all | solution.py:80
  245.4 99.0 %all-to-all-start.1 = ((bf16[8,4,256,512]{3,2,1,0:T(8,128)(2,1)}), bf16[8,4,256,512]{3,2,1,0:T(8,128)(2,1)}, u32[]{:S(2)}, u32[]{:S(2)}) async-start(bf16[8,4,256,512]{3,2,1,0:T(8,128)(2,1)} %broadcast_select_fusion), calls=%async_computation.1 | async-start | bytes 16777216 | tf_op jit(solution)/shard_map/all_to_all | solution.py:66
Sparse Core Ops, SparseCore 0:
  60.7 29.9 reduce-scatter.1
where the time goes:
time: 360 us; the launch traced here: 359 us
  waiting for transfers between devices  219 us (61%)
  local copies, waits for them, and re-layouts  44.1 us (12%)
  other arithmetic  26.5 us (7%)
  starting transfers between devices  24.6 us (7%)
  matrix products  21 us (6%)
  between operations  14.2 us (4%)
  blocking collectives  9.27 us (3%)
    all_to_all x1, waiting for transfers between devices, move_results(): lax.all_to_all(jnp.take(spread[0], matching, axis=0), 'section', split_ax...  92.7 us
    all_to_all x1, waiting for transfers between devices, move_results(): lax.all_to_all(fold_rows(updated_cache, groups), 'section', split_axis=0,...  91.8 us
    reduce_scatter x1, waiting for transfers between devices, decode_layer(): lax.psum_scatter(partial_value, 'tensor', scatter_dimension=1, tiled=True)  30 us
    unnamed x15, local copies, waits for them, and re-layouts  19.6 us
    select_n x2, other arithmetic, attend(): jnp.where(written[:, :, None], fresh_rows[:, None, :], cache_rows)  15 us
    dot_general x1, matrix products, decode_layer(): jnp.dot(attended, out_weight[0], preferred_element_type=jnp.float32)  14.6 us
    squeeze x1, local copies, waits for them, and re-layouts, decode_layer(): kv_cache[0]  12 us
    psum x1, blocking collectives, decode_layer(): lax.psum(jnp.sum(stream * stream, axis=-1, keepdims=True), 'tensor')  9.27 us
  transfers between devices with their start and end apart: 7, of which 4 were waited for; matrix products, arithmetic and copies ran while one was open for 8% of the time, Pallas kernels for 0%

commit v1 on v0

v1 whole, which is shorter than its diff:
```python
import functools
import itertools
import math
import random

import jax
import jax.numpy as jnp
import numpy as np
from jax import lax
from jax.experimental import pallas as pl
from jax.experimental.pallas import tpu as pltpu
from jax.sharding import PartitionSpec as P


D = 8192
HEAD_SIZE = 128
PIECES = 4
STREAMS = 2
MAX_ROUNDS = 8
BASE_ROUNDS = 4
FIELDS = 2 * MAX_ROUNDS + 8 * PIECES
RING = (0, 1, 3, 2)


def ring_path(source, target, clockwise):
    at = RING.index(source)
    hops = []
    while RING[at] != target:
        later = (at + (1 if clockwise else -1)) % 4
        hops.append((RING[at], RING[later]))
        at = later
    return hops


def demand_classes():
    pairs = [(a, b) for a in range(4) for b in range(a, 4)]
    return [
        combo
        for combo in itertools.product(pairs, repeat=4)
        if all(sum(pair.count(chip) for pair in combo) == 2 for chip in range(4))
    ]


def split_directions(items, rng):
    share = {}
    for source, which, target in items:
        gap = (RING.index(target) - RING.index(source)) % 4
        share[(source, which)] = {1: PIECES, 2: PIECES // 2, 3: 0}[gap]

    def cost():
        load = {}
        for source, which, target in items:
            count = share[(source, which)]
            for hop in ring_path(source, target, True):
                load[hop] = load.get(hop, 0) + count
            for hop in ring_path(source, target, False):
                load[hop] = load.get(hop, 0) + PIECES - count
        return (max(load.values(), default=0), sum(v * v for v in load.values()))

    keys = list(share)
    single = [((key, step),) for key in keys for step in (1, -1, 2, -2)]
    double = [
        ((key, a), (other, b))
        for key, other in itertools.combinations(keys, 2)
        for a in (1, -1)
        for b in (1, -1)
    ]
    best = cost()
    improved = True
    while improved:
        improved = False
        moves = single + double
        rng.shuffle(moves)
        for move in moves:
            if any(not 0 <= share[key] + step <= PIECES for key, step in move):
                continue
            for key, step in move:
                share[key] += step
            now = cost()
            if now < best:
                best = now
                improved = True
                break
            for key, step in move:
                share[key] -= step
    return (share, best[0])


def schedule_rounds(items, share, rng, noise):
    pieces = []
    for source, which, target in items:
        for number in range(PIECES):
            hops = ring_path(source, target, number < share[(source, which)])
            pieces.append([hops, 0, 0, (source, which, number)])
    rounds = []
    while any(piece[1] < len(piece[0]) for piece in pieces):
        taken = {}
        for piece in sorted(
            pieces, key=lambda piece: piece[1] - len(piece[0]) + noise * rng.random()
        ):
            if piece[1] < len(piece[0]) and piece[2] <= len(rounds):
                taken.setdefault(piece[0][piece[1]], piece)
        for piece in taken.values():
            piece[1] += 1
            piece[2] = len(rounds) + 1
        rounds.append({hop: piece[3] for hop, piece in taken.items()})
    return rounds


def solve_class(combo, tries=60):
    rng = random.Random(7)
    items = [
        (source, which, target)
        for source, pair in enumerate(combo)
        for which, target in enumerate(pair)
        if source != target
    ]
    best = None
    for attempt in range(tries):
        if attempt % 5 == 0:
            share, bound = split_directions(items, rng)
        rounds = schedule_rounds(items, share, rng, (0.5, 1.0, 1.0, 1.5, 2.5)[attempt % 5])
        if best is None or len(rounds) < len(best):
            best = rounds
        if len(best) <= bound:
            break
    assert len(best) <= MAX_ROUNDS
    return best


@functools.cache
def routing_tables():
    classes = demand_classes()
    index = np.zeros((1000,), np.int32)
    rows = np.zeros((len(classes), 2, 128), np.int32)
    for number, combo in enumerate(classes):
        ids = [lo * (7 - lo) // 2 + hi for lo, hi in combo]
        index[ids[0] + 10 * ids[1] + 100 * ids[2]] = number
        where = {
            (chip, which, piece): (chip, which * PIECES + piece)
            for chip in range(4)
            for which in range(2)
            for piece in range(PIECES)
        }
        flat = np.zeros((256,), np.int32)
        rounds = solve_class(combo)
        for step, taken in enumerate(rounds):
            for (source, target), piece in taken.items():
                across = 0 if source ^ target == 1 else 1
                chip, slot = where[piece]
                assert chip == source
                flat[source * FIELDS + 2 * step + across] = slot
                where[piece] = (target, 2 * PIECES + 2 * step + across)
        for (source, which, piece), (chip, slot) in where.items():
            assert chip == combo[source][which]
            flat[chip * FIELDS + 2 * MAX_ROUNDS + (source * 2 + which) * PIECES + piece] = slot
        flat[4 * FIELDS] = max(len(rounds), BASE_ROUNDS) - BASE_ROUNDS
        rows[number] = flat.reshape(2, 128)
    return (index, rows)


def route_kernel(place_ref, matching_ref, index_ref, rows_ref, out_ref, row, dest, swap, sem):
    place = place_ref[0]
    chip = place // 2
    core = place % 2
    for position in range(8):
        dest[matching_ref[position]] = position // 2
    key = 0
    for at in range(4):
        first, second = dest[2 * at], dest[2 * at + 1]
        swap[at] = (first > second).astype(jnp.int32)
        if at < 3:
            lo, hi = jnp.minimum(first, second), jnp.maximum(first, second)
            key = key + 10**at * (lo * (7 - lo) // 2 + hi)
    copy = pltpu.make_async_copy(rows_ref.at[index_ref[key]], row, sem)
    copy.start()
    copy.wait()

    def field(flat):
        return row[flat // 128, flat % 128]

    def local_id(slot):
        owner = (slot // PIECES) ^ swap[chip]
        near = jnp.where(owner == core, 0, PIECES) + slot % PIECES
        return jnp.where(slot < 2 * PIECES, near, slot)

    for step in range(2 * MAX_ROUNDS):
        out_ref[step] = local_id(field(chip * FIELDS + step))
    layer = matching_ref[place]
    which = (layer % 2) ^ swap[layer // 2]
    base = chip * FIELDS + 2 * MAX_ROUNDS + (layer // 2 * 2 + which) * PIECES
    for piece in range(PIECES):
        out_ref[2 * MAX_ROUNDS + piece] = local_id(field(base + piece))
    out_ref[2 * MAX_ROUNDS + PIECES] = field(jnp.int32(4 * FIELDS))


def find_route(place, matching):
    index, rows = routing_tables()
    smem = pl.BlockSpec(memory_space=pltpu.SMEM)
    return pl.pallas_call(
        route_kernel,
        out_shape=jax.ShapeDtypeStruct((32,), jnp.int32),
        in_specs=[smem, smem, smem, pl.BlockSpec(memory_space=pl.ANY)],
        out_specs=smem,
        scratch_shapes=[
            pltpu.SMEM((2, 128), jnp.int32),
            pltpu.SMEM((8,), jnp.int32),
            pltpu.SMEM((4,), jnp.int32),
            pltpu.SemaphoreType.DMA,
        ],
        name="find_route",
    )(place, matching, jnp.asarray(index), jnp.asarray(rows))


def write_kernel(
    rows, first_of, place_ref, lengths_ref, cache_ref, fresh_ref, out_ref, held, wide, sem_in, sem_out
):
    first = first_of(place_ref[0])

    def copy_in(row):
        return pltpu.make_async_copy(cache_ref.at[0, first + row], held.at[row], sem_in.at[row])

    def copy_out(row):
        return pltpu.make_async_copy(held.at[row], out_ref.at[row], sem_out.at[row])

    for row in range(rows):
        copy_in(row).start()
    wide[...] = fresh_ref[0].astype(jnp.float32)
    for row in range(rows):
        copy_in(row).wait()
        length = lengths_ref[first + row]
        start = pl.multiple_of(length // 16 * 16, 16)
        tile = held[row, pl.ds(start, 16), :].astype(jnp.float32)
        fresh = wide[pl.ds(first + row, 1), :]
        places = lax.broadcasted_iota(jnp.int32, tile.shape, 0) + start
        tile = jnp.where(places == length, fresh, tile)
        held[row, pl.ds(start, 16), :] = tile.astype(held.dtype)
        copy_out(row).start()
    for row in range(rows):
        copy_out(row).wait()


def write_tokens(place, lengths, kv_cache, fresh, rows, first_of):
    smem = pl.BlockSpec(memory_space=pltpu.SMEM)
    shape = (rows,) + kv_cache.shape[2:]
    return pl.pallas_call(
        functools.partial(write_kernel, rows, first_of),
        out_shape=jax.ShapeDtypeStruct(shape, kv_cache.dtype),
        in_specs=[
            smem,
            smem,
            pl.BlockSpec(memory_space=pl.ANY),
            pl.BlockSpec(memory_space=pltpu.VMEM),
        ],
        out_specs=pl.BlockSpec(memory_space=pl.ANY),
        scratch_shapes=[
            pltpu.VMEM(shape, kv_cache.dtype),
            pltpu.VMEM(fresh.shape[1:], jnp.float32),
            pltpu.SemaphoreType.DMA((rows,)),
            pltpu.SemaphoreType.DMA((rows,)),
        ],
        name="write_tokens",
        cost_estimate=pl.CostEstimate(
            flops=2 * math.prod(shape), bytes_accessed=4 * math.prod(shape), transcendentals=0
        ),
    )(place, lengths, kv_cache, fresh)


def pick_kernel(step, n_near, n_after, ids_ref, *refs):
    refs = refs[n_after:]
    near = refs[:n_near]
    per = refs[0].shape[0] // PIECES
    passed = (len(refs) - n_near - 6) // 2
    relays = (refs[n_near : n_near + passed], refs[n_near + passed : n_near + 2 * passed])
    outs = refs[-6:-4]
    held = refs[-4:-2]
    sem_in, sem_out = refs[-2:]
    for way in range(2):
        wanted = ids_ref[2 * step + way]
        for number, ref in enumerate(near):

            @pl.when((wanted >= number * PIECES) & (wanted < (number + 1) * PIECES))
            def _(number=number, ref=ref, wanted=wanted, way=way):
                start = (wanted - number * PIECES) * per
                pltpu.make_async_copy(ref.at[pl.ds(start, per)], held[way], sem_in.at[way]).start()

        for past, ref in enumerate(relays[way]):

            @pl.when(wanted == 2 * PIECES + 2 * past + 1 - way)
            def _(ref=ref, way=way):
                pltpu.make_async_copy(ref, held[way], sem_in.at[way]).start()

    def copy_out(way):
        return pltpu.make_async_copy(held[way], outs[way], sem_out.at[way])

    for way in range(2):
        pltpu.make_async_copy(near[0].at[pl.ds(0, per)], held[way], sem_in.at[way]).wait()
        copy_out(way).start()
    for way in range(2):
        copy_out(way).wait()


def pick_pieces(ids, step, near, from_x, from_y, after=()):
    shape = (near[0].shape[0] // PIECES,) + near[0].shape[1:]
    held = pltpu.VMEM(shape, near[0].dtype)
    anywhere = pl.BlockSpec(memory_space=pl.ANY)
    operands = list(after) + list(near) + list(from_y) + list(from_x)
    one = jax.ShapeDtypeStruct(shape, near[0].dtype)
    return pl.pallas_call(
        functools.partial(pick_kernel, step, len(near), len(after)),
        out_shape=(one, one),
        in_specs=[pl.BlockSpec(memory_space=pltpu.SMEM)] + [anywhere] * len(operands),
        out_specs=(anywhere, anywhere),
        scratch_shapes=[
            held,
            held,
            pltpu.SemaphoreType.DMA((2,)),
            pltpu.SemaphoreType.DMA((2,)),
        ],
        name="pick_pieces",
        cost_estimate=pl.CostEstimate(
            flops=2 * math.prod(shape), bytes_accessed=8 * math.prod(shape), transcendentals=0
        ),
    )(ids, *operands)


def place_kernel(lo, hi, per, layout, place_ref, ids_ref, *refs):
    out_ref, held, sem_in, sem_out = refs[-4:]
    core = place_ref[0] % 2
    blocks = [
        (side, stream, piece)
        for stream in range(STREAMS)
        for side in range(2)
        for piece in range(PIECES)
    ]

    def row_of(side, stream, piece):
        half = core if side == 0 else 1 - core
        return half * (STREAMS * PIECES * per) + (stream * PIECES + piece) * per

    def move(at, side, stream, piece):
        wanted = ids_ref[2 * MAX_ROUNDS + piece]
        mine = (wanted >= lo) & (wanted < hi)
        for number in range(2):
            if lo < 2 * PIECES:

                @pl.when((wanted >= number * PIECES) & (wanted < (number + 1) * PIECES))
                def _(ref=refs[layout["near"][side][number][stream]]):
                    start = (wanted - number * PIECES) * per
                    pltpu.make_async_copy(
                        ref.at[pl.ds(start, per)], held.at[at], sem_in.at[at]
                    ).start()

        for slot, position in layout["far"][side][stream].items():
            if lo <= slot < hi:

                @pl.when(wanted == slot)
                def _(ref=refs[position]):
                    pltpu.make_async_copy(ref, held.at[at], sem_in.at[at]).start()

        return mine

    def copy_out(at, block):
        row = row_of(*block)
        return pltpu.make_async_copy(held.at[at], out_ref.at[0, pl.ds(row, per)], sem_out.at[at])

    mine = [move(at, *block) for at, block in enumerate(blocks)]
    for at, block in enumerate(blocks):

        @pl.when(mine[at])
        def _(at=at, block=block):
            pltpu.make_async_copy(
                out_ref.at[0, pl.ds(0, per)], held.at[at], sem_in.at[at]
            ).wait()
            copy_out(at, block).start()

    for at, block in enumerate(blocks):

        @pl.when(mine[at])
        def _(at=at, block=block):
            copy_out(at, block).wait()


def place_pieces(place, ids, lo, hi, near, far, result, out_shape, after=()):
    operands = []
    layout = {"near": [[[0, 0] for _ in range(2)] for _ in range(2)], "far": [[{}, {}], [{}, {}]]}

    def add(array):
        operands.append(array)
        return len(operands) - 1

    for side in range(2):
        for stream in range(STREAMS):
            if lo < 2 * PIECES:
                for owner in range(2):
                    layout["near"][side][owner][stream] = add(near[side][owner][stream])
            for slot, array in far[side][stream].items():
                if lo <= slot < hi:
                    layout["far"][side][stream][slot] = add(array)
    per = out_shape.shape[1] // (2 * STREAMS * PIECES)
    smem = pl.BlockSpec(memory_space=pltpu.SMEM)
    anywhere = pl.BlockSpec(memory_space=pl.ANY)
    operands += list(after)
    aliases = {}
    if result is not None:
        aliases = {2 + len(operands): 0}
        operands.append(result)
    count = 2 * STREAMS * PIECES
    return pl.pallas_call(
        functools.partial(place_kernel, lo, hi, per, layout),
        out_shape=out_shape,
        in_specs=[smem, smem] + [anywhere] * len(operands),
        out_specs=anywhere,
        scratch_shapes=[
            pltpu.VMEM((count, per) + out_shape.shape[2:], out_shape.dtype),
            pltpu.SemaphoreType.DMA((count,)),
            pltpu.SemaphoreType.DMA((count,)),
        ],
        input_output_aliases=aliases,
        name="place_pieces",
        cost_estimate=pl.CostEstimate(
            flops=math.prod(out_shape.shape),
            bytes_accessed=2 * math.prod(out_shape.shape),
            transcendentals=0,
        ),
    )(place, ids, *operands)


def attend_kernel(block, lengths_ref, q_ref, cache_ref, fresh_ref, *refs):
    out_ref = refs[-1]
    base = pl.program_id(0) * block
    slots = cache_ref.shape[2]
    per_key = q_ref.shape[1]
    scores = []
    for row in range(block):
        length = lengths_ref[base + row]
        key = cache_ref[0, row, :, :HEAD_SIZE]
        query = q_ref[row]
        fresh_key = fresh_ref[0, row : row + 1, :HEAD_SIZE]
        s = lax.dot_general(
            query, key, (((1,), (1,)), ((), ())), preferred_element_type=jnp.float32
        )
        new = jnp.sum(
            query.astype(jnp.float32) * fresh_key.astype(jnp.float32), axis=1, keepdims=True
        )
        spots = lax.broadcasted_iota(jnp.int32, (per_key, slots), 1)
        s = jnp.where(spots == length, new, s) / math.sqrt(HEAD_SIZE)
        scores.append(jnp.where(spots <= length, s, -1e30))
    scores = jnp.stack(scores)
    scores = jnp.exp(scores - jnp.max(scores, axis=-1, keepdims=True))
    weights = scores / jnp.sum(scores, axis=-1, keepdims=True)
    for row in range(block):
        length = lengths_ref[base + row]
        weight = weights[row].astype(jnp.bfloat16)
        wide = weight.astype(jnp.float32)
        spots = lax.broadcasted_iota(jnp.int32, (per_key, slots), 1)
        at_new = jnp.sum(jnp.where(spots == length, wide, 0.0), axis=1, keepdims=True)
        rest = jnp.where(spots == length, 0.0, wide).astype(jnp.bfloat16)
        value = cache_ref[0, row, :, HEAD_SIZE:]
        fresh_value = fresh_ref[0, row : row + 1, HEAD_SIZE:].astype(jnp.float32)
        total = jnp.dot(rest, value, preferred_element_type=jnp.float32)
        out_ref[row] = (total + at_new * fresh_value).astype(out_ref.dtype)


def attend(head, lengths, queries, kv_cache, fresh, after=()):
    block = 8
    rows, slots = kv_cache.shape[1:3]
    kv_heads = kv_cache.shape[3] // (2 * HEAD_SIZE)
    per_key = queries.shape[1] // kv_heads
    work = rows * per_key * slots * HEAD_SIZE
    return pl.pallas_call(
        functools.partial(attend_kernel, block),
        out_shape=jax.ShapeDtypeStruct((rows, per_key, HEAD_SIZE), jnp.bfloat16),
        grid_spec=pltpu.PrefetchScalarGridSpec(
            num_scalar_prefetch=1,
            grid=(rows // block,),
            in_specs=[
                pl.BlockSpec((block, per_key, HEAD_SIZE), lambda i, _: (i, head, 0)),
                pl.BlockSpec((1, block, slots, 2 * HEAD_SIZE), lambda i, _: (0, i, 0, head)),
                pl.BlockSpec((1, block, 2 * HEAD_SIZE), lambda i, _: (0, i, head)),
            ]
            + [pl.BlockSpec(memory_space=pl.ANY)] * len(after),
            out_specs=pl.BlockSpec((block, per_key, HEAD_SIZE), lambda i, _: (i, 0, 0)),
        ),
        name="attend",
        cost_estimate=pl.CostEstimate(
            flops=30 * work, bytes_accessed=rows * slots * 4 * HEAD_SIZE, transcendentals=0
        ),
    )(lengths, queries, kv_cache, fresh, *after)


def shift_pairs(size, shift):
    return [(at, (at + shift) % size) for at in range(size)]


def flip_pairs(size, mask):
    return [(at, at ^ mask) for at in range(size)]


def sum_over_tensor(value):
    size = lax.axis_size("tensor")
    total = value
    for shift in range(1, size):
        total = total + lax.ppermute(value, "tensor", shift_pairs(size, shift))
    return total


def scatter_sum(partial_value):
    size = lax.axis_size("tensor")
    parts = lax.all_to_all(partial_value, "tensor", split_axis=1, concat_axis=0, tiled=True)
    return jnp.sum(parts.reshape((size,) + (partial_value.shape[0], -1)), axis=0)


def norm_rows(stream, norm_gain):
    squares = sum_over_tensor(jnp.sum(stream * stream, axis=-1, keepdims=True))
    normed = stream * lax.rsqrt(squares / D + 1e-05) * norm_gain[0].astype(jnp.float32)
    return jnp.concatenate([stream.astype(jnp.bfloat16), normed.astype(jnp.bfloat16)], axis=1)


def spread_rows(matching, value):
    groups = lax.axis_size("section")
    folded = value.reshape((groups, value.shape[0] // groups) + value.shape[1:])
    spread = lax.all_to_all(folded, "section", split_axis=0, concat_axis=0, tiled=True)
    return jnp.take(spread, matching, axis=0, mode="clip")


def gather_rows(chosen, shape):
    landed = lax.all_to_all(chosen, "section", split_axis=0, concat_axis=0, tiled=True)
    return landed.reshape(shape)


def move_by_two_exchanges(matching, value):
    return gather_rows(spread_rows(matching, value), value.shape)


def on_any_section(
    matching, lengths, queries, kv_cache, incoming_key_value, residual, out_weight, norm_gain
):
    place = lax.axis_index("section").astype(jnp.int32).reshape(1)
    rows = kv_cache.shape[1]
    updated = write_tokens(
        place, lengths, kv_cache, incoming_key_value, rows, lambda _: 0
    )
    cache_out = move_by_two_exchanges(matching, updated)
    kv_heads = kv_cache.shape[3] // (2 * HEAD_SIZE)
    split_queries = queries.reshape(rows, -1, HEAD_SIZE)
    partial_value = 0.0
    depth = out_weight.shape[1] // kv_heads
    for head in range(kv_heads):
        attended = attend(head, lengths, split_queries, kv_cache, incoming_key_value)
        partial_value += jnp.dot(
            attended.reshape(rows, -1),
            out_weight[0, head * depth : (head + 1) * depth],
            preferred_element_type=jnp.float32,
        )
    stream = residual[0].astype(jnp.float32) + scatter_sum(partial_value)
    both = norm_rows(stream, norm_gain)
    both = move_by_two_exchanges(matching, both)
    width = both.shape[1] // 2
    return (cache_out[None], both[None, :, :width], both[None, :, width:])


def on_four_chips(
    matching, lengths, queries, kv_cache, incoming_key_value, residual, out_weight, norm_gain
):
    place = lax.axis_index("section").astype(jnp.int32).reshape(1)
    sections = lax.axis_size("section")
    across_core, across_x, across_y = (flip_pairs(sections, mask) for mask in (1, 2, 4))
    rows = kv_cache.shape[1]
    kv_heads = kv_cache.shape[3] // (2 * HEAD_SIZE)
    fresh = incoming_key_value
    part = rows // (2 * STREAMS)

    def swap(array):
        return lax.ppermute(array, "section", across_core)

    lent, kept, got = [], [], []
    for stream in range(STREAMS):
        lent.append(
            write_tokens(
                place, lengths, kv_cache, fresh, part,
                lambda p, s=stream: (1 - p % 2) * (rows // 2) + s * part,
            )
        )
        got.append(swap(lent[-1]))
    ids = find_route(place, matching)
    for stream in range(STREAMS):
        kept.append(
            write_tokens(
                place, lengths, kv_cache, fresh, part,
                lambda p, s=stream: p % 2 * (rows // 2) + s * part,
            )
        )

    from_x = [[] for _ in range(STREAMS)]
    from_y = [[] for _ in range(STREAMS)]
    far = [[{} for _ in range(STREAMS)] for _ in range(2)]

    def send(step, stream, from_x, from_y, kept, got, ids, after=()):
        out_x, out_y = pick_pieces(
            ids, step, (kept[stream], got[stream]), from_x[stream], from_y[stream], after
        )
        landed_x = lax.ppermute(out_x, "section", across_x)
        landed_y = lax.ppermute(out_y, "section", across_y)
        return ((landed_x, landed_y), out_x)

    def receive(step, stream, landed, from_x, from_y, far):
        for way, array in enumerate(landed):
            (from_x, from_y)[way][stream].append(array)
            slot = 2 * PIECES + 2 * step + way
            far[0][stream][slot] = array
            far[1][stream][slot] = swap(array)

    split_queries = queries.reshape(rows, -1, HEAD_SIZE)
    depth = out_weight.shape[1] // kv_heads
    work = {}

    def attend_head(head):
        work["attended"] = attend(
            head, lengths, split_queries, kv_cache, incoming_key_value, [work["sent"]]
        )
        return [work["attended"]]

    def project_head(head):
        product = jnp.dot(
            work["attended"].reshape(rows, -1),
            out_weight[0, head * depth : (head + 1) * depth],
            preferred_element_type=jnp.float32,
        )
        work["partial"] = product if head == 0 else work["partial"] + product
        return [work["partial"]]

    def add_parts():
        work["stream"] = residual[0].astype(jnp.float32) + scatter_sum(work["partial"])
        return [work["stream"]]

    def norm_stream():
        work["both"] = norm_rows(work["stream"], norm_gain)
        return [work["both"]]

    def spread_both():
        work["chosen"] = spread_rows(matching, work["both"])
        return [work["chosen"]]

    def gather_both():
        work["moved"] = gather_rows(work["chosen"], work["both"].shape)
        return [work["moved"]]

    chores = []
    for head in range(kv_heads):
        chores += [functools.partial(attend_head, head), functools.partial(project_head, head)]
    chores += [add_parts, norm_stream, spread_both, gather_both]
    after = []
    for step in range(BASE_ROUNDS):
        for stream in range(STREAMS):
            settled = [far[1][stream][s] for s in far[1][stream] if s < 2 * PIECES + 2 * step - 2]
            landed, work["sent"] = send(
                step, stream, from_x, from_y, kept, got, ids, after + settled[-2:]
            )
            receive(step, stream, landed, from_x, from_y, far)
            after = []
            if step + stream > 0 and chores:
                after = chores.pop(0)()
    for chore in chores:
        after = chore()
    lent_back = [swap(array) for array in kept]
    near = [[kept, got], [lent, lent_back]]
    both = work["moved"]
    out_shape = jax.ShapeDtypeStruct(kv_cache.shape, kv_cache.dtype)
    ready = 2 * PIECES + 2 * (BASE_ROUNDS - 1)
    result = place_pieces(place, ids, 0, ready, near, far, None, out_shape, after)

    def finish(extra, place, ids, kept, got, from_x, from_y, far, result):
        from_x, from_y = [list(a) for a in from_x], [list(a) for a in from_y]
        far = [[dict(a) for a in side] for side in far]
        lo = ready
        for step in range(BASE_ROUNDS, BASE_ROUNDS + extra):
            for stream in range(STREAMS):
                landed, _ = send(step, stream, from_x, from_y, kept, got, ids)
                receive(step, stream, landed, from_x, from_y, far)
        if extra:
            mid = 2 * PIECES + 2 * (BASE_ROUNDS + extra - 1)
            result = place_pieces(place, ids, lo, mid, None, far, result, out_shape)
            lo = mid
        top = 2 * PIECES + 2 * (BASE_ROUNDS + extra)
        return place_pieces(place, ids, lo, top, None, far, result, out_shape)

    late = [[{s: a for s, a in d.items() if s >= ready} for d in side] for side in far]
    cache_out = lax.switch(
        ids[2 * MAX_ROUNDS + PIECES],
        [functools.partial(finish, extra) for extra in range(MAX_ROUNDS - BASE_ROUNDS + 1)],
        place, ids, kept, got, from_x, from_y, late, result,
    )
    width = both.shape[1] // 2
    return (cache_out, both[None, :, :width], both[None, :, width:])


def solution(mesh):
    four_chips = mesh.shape["section"] == 8
    return jax.shard_map(
        on_four_chips if four_chips else on_any_section,
        mesh=mesh,
        in_specs=(
            P(),
            P(),
            P("section", None, "tensor"),
            P("section", None, None, "tensor"),
            P("section", None, "tensor"),
            P("section", None, "tensor"),
            P("section", "tensor", None),
            P("section", "tensor"),
        ),
        out_specs=(
            P("section", None, None, "tensor"),
            P("section", None, "tensor"),
            P("section", None, "tensor"),
        ),
        check_vma=False,
    )
```

time: 360 us -> 218 us (0.61)
  waiting for transfers between devices: 219 us -> 68.6 us
  Pallas kernels: 0 us -> 61.2 us
  local copies, waits for them, and re-layouts: 44.1 us -> 11.5 us
  starting transfers between devices: 24.6 us -> 44.6 us
  other arithmetic: 26.5 us -> 9.19 us
  between operations: 14.2 us -> 1.79 us
  blocking collectives: 9.27 us -> 0 us
    all_to_all x6 -> x3, waiting for transfers between devices: 189 us -> 25.1 us  [the longest x1 20.7 us: spread_rows(): lax.all_to_all(folded, 'section', split_axis=0, concat_axis=0, tiled=True)]
    pallas_call x0 -> x20, Pallas kernels: none -> 61.2 us  [the longest x10 25.3 us: pick_pieces(): pl.pallas_call(functools.partial(pick_kernel, step, len(near), len(after)...]
    ppermute x0 -> x47, waiting for transfers between devices: none -> 43.5 us  [the longest x10 33.1 us: send(): landed_x = lax.ppermute(out_x, 'section', across_x)]
    ppermute x0 -> x47, starting transfers between devices: none -> 32 us  [the longest x10 11.2 us: send(): landed_y = lax.ppermute(out_y, 'section', across_y)]
    reduce_scatter x1 -> x0, waiting for transfers between devices: 30 us -> none  [decode_layer(): lax.psum_scatter(partial_value, 'tensor', scatter_dimension=1, tiled=True)]
    select_n x5 -> x0, other arithmetic: 23.5 us -> none  [the longest x2 15 us: attend(): jnp.where(written[:, :, None], fresh_rows[:, None, :], cache_rows)]
    unnamed x15 -> x31, local copies, waits for them, and re-layouts: 19.6 us -> 3.28 us
    squeeze x1 -> x0, local copies, waits for them, and re-layouts: 12 us -> none  [decode_layer(): kv_cache[0]]
  transfers between devices with their start and end apart: 7 -> 50, of which waited for: 4 -> 13; matrix products, arithmetic and copies ran while one was open for 8% -> 17% of each run, Pallas kernels for 0% -> 25%
where the time goes in v1:
time: 218 us; the launch traced here: 216 us
  waiting for transfers between devices  68.6 us (31%)
  Pallas kernels  61.2 us (28%)
  starting transfers between devices  44.6 us (20%)
  matrix products  18.8 us (9%)
  local copies, waits for them, and re-layouts  11.5 us (5%)
  other arithmetic  9.19 us (4%)
    ppermute x10, waiting for transfers between devices, send(): landed_x = lax.ppermute(out_x, 'section', across_x)  33.1 us
    pallas_call x10, Pallas kernels, pick_pieces(): pl.pallas_call(functools.partial(pick_kernel, step, len(near), len(after)...  25.3 us
    all_to_all x1, waiting for transfers between devices, spread_rows(): lax.all_to_all(folded, 'section', split_axis=0, concat_axis=0, tiled=True)  20.7 us
    dot_general x2, matrix products, project_head(): jnp.dot(work['attended'].reshape(rows, -1), out_weight[0, head * depth:(h...  18.8 us
    pallas_call x4, Pallas kernels, write_tokens(): pl.pallas_call(functools.partial(write_kernel, rows, first_of), out_shape...  12.2 us
    ppermute x10, starting transfers between devices, send(): landed_y = lax.ppermute(out_y, 'section', across_y)  11.2 us
    pallas_call x2, Pallas kernels, attend(): pl.pallas_call(functools.partial(attend_kernel, block), out_shape=jax.Sha...  11 us
    ppermute x10, starting transfers between devices, send(): landed_x = lax.ppermute(out_x, 'section', across_x)  10.7 us
  transfers between devices with their start and end apart: 50, of which 13 were waited for; matrix products, arithmetic and copies ran while one was open for 17% of the time, Pallas kernels for 25%

profile of v1, /device:TPU:0, one launch (start us, length us, event | category | flops | bytes accessed | tf_op | source)
XLA Modules:
  0.0 215.8 jit_solution(13030421603430796976)
XLA Ops:
  0.6 3.2 %write_tokens.5.refs_24_ = bf16[8,256,512]{2,1,0:T(8,128)(2,1)} custom-call(s32[1]{0:T(128)} %bitcast.place_ref, s32[32]{0:T(128)} %lengths_ref.11, bf16[1,32,256,512]{3,2,1,0:T(8,128)(2,1)} %cache_ref.11, bf16[1,32,512]{2,1,0:T(8,128)(2,1)} %fresh_ref.11), custom_call_target="tpu_custom_call" | custom-call | flops 2097152 | bytes 4194304 | tf_op jit(solution)/shard_map/write_tokens/pallas_call | solution.py:246
  4.4 3.3 %write_tokens.7.refs_16_ = bf16[8,256,512]{2,1,0:T(8,128)(2,1)} custom-call(s32[1]{0:T(128)} %bitcast.place_ref, s32[32]{0:T(128)} %lengths_ref.11, bf16[1,32,256,512]{3,2,1,0:T(8,128)(2,1)} %cache_ref.11, bf16[1,32,512]{2,1,0:T(8,128)(2,1)} %fresh_ref.11), custom_call_target="tpu_custom_call" | custom-call | flops 2097152 | bytes 4194304 | tf_op jit(solution)/shard_map/write_tokens/pallas_call | solution.py:246
  13.3 3.2 %write_tokens.6.refs_0_.refs_1_.refs_3_ = bf16[8,256,512]{2,1,0:T(8,128)(2,1)} custom-call(s32[1]{0:T(128)} %bitcast.place_ref, s32[32]{0:T(128)} %lengths_ref.11, bf16[1,32,256,512]{3,2,1,0:T(8,128)(2,1)} %cache_ref.11, bf16[1,32,512]{2,1,0:T(8,128)(2,1)} %fresh_ref.11), custom_call_target="tpu_custom_call" | custom-call | flops 2097152 | bytes 4194304 | tf_op jit(solution)/shard_map/write_tokens/pallas_call | solution.py:246
  19.2 3.0 %collective-permute-start.82 = (bf16[2,256,512]{2,1,0:T(8,128)(2,1)}, bf16[2,256,512]{2,1,0:T(8,128)(2,1)S(1)}, u32[]{:S(2)}, u32[]{:S(2)}) collective-permute-start(bf16[2,256,512]{2,1,0:T(8,128)(2,1)} %get-tuple-element.422.refs_0_), channel_id=1, source_target_pairs={{0,8},{4,12},{8,0},{12,4},{16,24},{20,28},{24,16},{28,20},{1,9},{5... | collective-permute-start | bytes 1572872 | tf_op jit(solution)/shard_map/ppermute | solution.py:603
  23.7 5.5 %attend.2.refs_0_ = bf16[32,8,128]{2,1,0:T(8,128)(2,1)} custom-call(s32[32]{0:T(128)} %lengths_ref.11, bf16[32,16,128]{2,1,0:T(8,128)(2,1)} %bitcast.40, bf16[1,32,256,512]{3,2,1,0:T(8,128)(2,1)} %cache_ref.11, bf16[1,32,512]{2,1,0:T(8,128)(2,1)} %fresh_ref.11, bf16[2,256,512]{2,1,0:T(8,128)(2,1)} %get-tuple-element.422.refs_0_), custom_call_target="tpu_custom_call" | custom-call | flops 251658240 | bytes 4194304 | tf_op jit(solution)/shard_map/attend/pallas_call | solution.py:471
  32.5 9.8 %fusion.2.refs_0_ = f32[32,8192]{1,0:T(8,128)} fusion(bf16[1,2048,8192]{2,1,0:T(8,128)(2,1)} %param.21, bf16[4,8,8,128]{3,2,1,0:T(8,128)(2,1)} %bitcast.43), kind=kOutput, calls=%fused_computation.3 | convolution fusion | flops 536870912 | bytes 17891328 | tf_op jit(solution)/shard_map/dot_general | solution.py:625
  42.3 2.7 %pick_pieces.49 = (bf16[2,256,512]{2,1,0:T(8,128)(2,1)}, bf16[2,256,512]{2,1,0:T(8,128)(2,1)}) custom-call(s32[32]{0:T(128)S(1)} %find_route.1.ids_ref, f32[32,8192]{1,0:T(8,128)} %fusion.2.refs_0_, bf16[8,256,512]{2,1,0:T(8,128)(2,1)S(1)} %write_tokens.4.refs_0_.refs_1_.refs_3_.refs_8_, ...), custom_call_target="tpu_custom_call" | custom-call | flops 524288 | bytes 2097152 | tf_op jit(solution)/shard_map/pick_pieces/pallas_call | solution.py:309
  45.0 5.5 %attend.3.refs_0_ = bf16[32,8,128]{2,1,0:T(8,128)(2,1)} custom-call(s32[32]{0:T(128)} %lengths_ref.11, bf16[32,16,128]{2,1,0:T(8,128)(2,1)} %bitcast.41, bf16[1,32,256,512]{3,2,1,0:T(8,128)(2,1)} %cache_ref.11, bf16[1,32,512]{2,1,0:T(8,128)(2,1)} %fresh_ref.11, bf16[2,256,512]{2,1,0:T(8,128)(2,1)} %get-tuple-element.424.refs_0_), custom_call_target="tpu_custom_call" | custom-call | flops 251658240 | bytes 4194304 | tf_op jit(solution)/shard_map/attend/pallas_call | solution.py:471
  50.5 9.0 %fusion.6.refs_0_ = f32[32,8192]{1,0:T(8,128)S(1)} fusion(f32[32,8192]{1,0:T(8,128)} %fusion.2.refs_0_, bf16[1,2048,8192]{2,1,0:T(8,128)(2,1)} %param.21, bf16[4,8,8,128]{3,2,1,0:T(8,128)(2,1)} %bitcast.42), kind=kOutput, calls=%fused_computation.7 | convolution fusion | flops 537133056 | bytes 18939904 | tf_op jit(solution)/shard_map/dot_general | solution.py:625
  61.5 5.3 %all-to-all-start = ((f32[32,4,2048]{2,0,1:T(8,128)}), f32[32,4,2048]{2,0,1:T(8,128)}, u32[]{:S(2)}, u32[]{:S(2)}) async-start(f32[32,4,2048]{2,0,1:T(8,128)} %bitcast.39), calls=%async_computation | async-start | bytes 2097152 | tf_op jit(solution)/shard_map/all_to_all | solution.py:510
  73.5 8.7 %collective-permute-done.86.refs_8_.refs_9_.refs_4_ = bf16[2,256,512]{2,1,0:T(8,128)(2,1)S(1)} collective-permute-done((bf16[2,256,512]{2,1,0:T(8,128)(2,1)}, bf16[2,256,512]{2,1,0:T(8,128)(2,1)S(1)}, u32[]{:S(2)}, u32[]{:S(2)}) %collective-permute-start.86) | collective-permute-done | bytes 524320 | tf_op jit(solution)/shard_map/ppermute | solution.py:603
  82.6 3.4 %collective-permute-done.88.refs_6_.refs_5_ = bf16[2,256,512]{2,1,0:T(8,128)(2,1)S(1)} collective-permute-done((bf16[2,256,512]{2,1,0:T(8,128)(2,1)}, bf16[2,256,512]{2,1,0:T(8,128)(2,1)S(1)}, u32[]{:S(2)}, u32[]{:S(2)}) %collective-permute-start.88) | collective-permute-done | bytes 524320 | tf_op jit(solution)/shard_map/ppermute | solution.py:604
  87.6 2.7 %pick_pieces.52 = (bf16[2,256,512]{2,1,0:T(8,128)(2,1)}, bf16[2,256,512]{2,1,0:T(8,128)(2,1)}) custom-call(s32[32]{0:T(128)S(1)} %find_route.1.ids_ref, bf16[32,8,128]{2,1,0:T(8,128)(2,1)} %attend.3.refs_0_, bf16[2,256,512]{2,1,0:T(8,128)(2,1)} %copy-done.8, bf16[2,256,512]{2,1,0:T(8,128)(2,1)} %collective-permute-done.91.refs_2_.refs_19_, ...), custom_call_target="tpu_custom_call" | custom-call | flops 524288 | bytes 2097152 | tf_op jit(solution)/shard_map/pick_pieces/pallas_call | solution.py:309
  90.9 3.6 %collective-permute-done.101.refs_6_.refs_13_ = bf16[2,256,512]{2,1,0:T(8,128)(2,1)} collective-permute-done((bf16[2,256,512]{2,1,0:T(8,128)(2,1)}, bf16[2,256,512]{2,1,0:T(8,128)(2,1)}, u32[]{:S(2)}, u32[]{:S(2)}) %collective-permute-start.101) | collective-permute-done | bytes 524320 | tf_op jit(solution)/shard_map/ppermute | solution.py:604
  103.0 3.5 %collective-permute-done.93.refs_10_.refs_6_ = bf16[2,256,512]{2,1,0:T(8,128)(2,1)} collective-permute-done((bf16[2,256,512]{2,1,0:T(8,128)(2,1)}, bf16[2,256,512]{2,1,0:T(8,128)(2,1)}, u32[]{:S(2)}, u32[]{:S(2)}) %collective-permute-start.93) | collective-permute-done | bytes 524320 | tf_op jit(solution)/shard_map/ppermute | solution.py:603
  137.8 3.7 %all-to-all-start.1 = ((bf16[8,4,4096]{2,1,0:T(4,128)(2,1)}), bf16[8,4,4096]{2,1,0:T(4,128)(2,1)S(1)}, u32[]{:S(2)}, u32[]{:S(2)}) async-start(bf16[8,4,4096]{2,1,0:T(4,128)(2,1)} %pad_maximum_fusion.1), calls=%async_computation.1 | async-start | bytes 524288 | tf_op jit(solution)/shard_map/all_to_all | solution.py:523
  141.5 20.7 %all-to-all-done.1 = bf16[8,4,4096]{2,1,0:T(4,128)(2,1)S(1)} async-done(((bf16[8,4,4096]{2,1,0:T(4,128)(2,1)}), bf16[8,4,4096]{2,1,0:T(4,128)(2,1)S(1)}, u32[]{:S(2)}, u32[]{:S(2)}) %all-to-all-start.1) | async-done | bytes 262176 | tf_op jit(solution)/shard_map/all_to_all | solution.py:523
  163.7 3.6 %all-to-all-start.2 = ((bf16[8,4,4096]{2,1,0:T(4,128)(2,1)}), bf16[8,4,4096]{2,1,0:T(4,128)(2,1)S(1)}, u32[]{:S(2)}, u32[]{:S(2)}) async-start(bf16[8,4,4096]{2,1,0:T(4,128)(2,1)} %gather_fusion), calls=%async_computation.2 | async-start | bytes 524288 | tf_op jit(solution)/shard_map/all_to_all | solution.py:528
  169.7 4.3 %all-to-all-done.2 = bf16[8,4,4096]{2,1,0:T(4,128)(2,1)S(1)} async-done(((bf16[8,4,4096]{2,1,0:T(4,128)(2,1)}), bf16[8,4,4096]{2,1,0:T(4,128)(2,1)S(1)}, u32[]{:S(2)}, u32[]{:S(2)}) %all-to-all-start.2) | async-done | bytes 262176 | tf_op jit(solution)/shard_map/all_to_all | solution.py:528
  174.7 6.1 %place_pieces.19 = bf16[1,32,256,512]{3,2,1,0:T(8,128)(2,1)} custom-call(s32[1]{0:T(128)} %bitcast.place_ref, s32[32]{0:T(128)S(1)} %find_route.1.ids_ref, bf16[8,256,512]{2,1,0:T(8,128)(2,1)} %write_tokens.6.refs_0_.refs_1_.refs_3_, bf16[8,256,512]{2,1,0:T(8,128)(2,1)} %collective-permute-done.83.refs_1_.refs_2_.refs_4_, ...), custom_call_target="tpu_custom_call" | custom-call | flops 4194304 | bytes 8388608 | tf_op jit(solution)/shard_map/place_pieces/pallas_call | solution.py:409
  181.6 34.0 %conditional.1 = (bf16[1,32,256,512]{3,2,1,0:T(8,128)(2,1)}) conditional(s32[]{:T(128)} %bitcast.1, (s32[1]{0:T(128)}, s32[32]{0:T(128)S(1)}, bf16[2,256,512]{2,1,0:T(8,128)(2,1)S(1)}, bf16[2,256,512]{2,1,0:T(8,128)(2,1)S(1)}, bf16[2,256,512]{2,1,0:T(8,128)(2,1)}, /*index=5*/bf16[2,256,512]{2,1,0:T(8,128)(2,1)}, ...), branch_computations={%region_2.3_spmd, %region_3.4_spmd, %region_4.5_spmd, %region_5.6_... | conditional | flops 12582912 | bytes 109053312 | solution.py:689
  190.1 9.4 %collective-permute-done.refs_0_ = bf16[2,256,512]{2,1,0:T(8,128)(2,1)} collective-permute-done((bf16[2,256,512]{2,1,0:T(8,128)(2,1)}, bf16[2,256,512]{2,1,0:T(8,128)(2,1)}, u32[]{:S(2)}, u32[]{:S(2)}) %collective-permute-start) | collective-permute-done | bytes 524320 | tf_op jit(solution)/shard_map/cond/branch_1_fun/ppermute | solution.py:603
  200.3 9.5 %collective-permute-done.2.refs_2_ = bf16[2,256,512]{2,1,0:T(8,128)(2,1)S(1)} collective-permute-done((bf16[2,256,512]{2,1,0:T(8,128)(2,1)}, bf16[2,256,512]{2,1,0:T(8,128)(2,1)S(1)}, u32[]{:S(2)}, u32[]{:S(2)}) %collective-permute-start.2) | collective-permute-done | bytes 524320 | tf_op jit(solution)/shard_map/cond/branch_1_fun/ppermute | solution.py:603
  210.4 3.3 %place_pieces.11.refs_8_ = bf16[1,32,256,512]{3,2,1,0:T(8,128)(2,1)} custom-call(s32[1]{0:T(128)} %get-tuple-element.255.place_ref, s32[32]{0:T(128)S(1)} %get-tuple-element.256.ids_ref, bf16[2,256,512]{2,1,0:T(8,128)(2,1)S(1)} %get-tuple-element.266.refs_9_.refs_0_, ...), custom_call_target="tpu_custom_call", output_to_operand_aliasing={{}: (10, {})} | custom-call | flops 4194304 | bytes 8388608 | tf_op jit(solution)/shard_map/cond/branch_1_fun/place_pieces/pallas_call | solution.py:409
  (157 shorter events, 80.8 us)
Async XLA Ops:
  7.7 21.5 %collective-permute-start.83 = (bf16[8,256,512]{2,1,0:T(8,128)(2,1)}, bf16[8,256,512]{2,1,0:T(8,128)(2,1)}, u32[]{:S(2)}, u32[]{:S(2)}) collective-permute-start(bf16[8,256,512]{2,1,0:T(8,128)(2,1)} %write_tokens.7.refs_16_), channel_id=1, source_target_pairs={{0,4},{4,0},{8,12},{12,8},{16,20},{20,16},{24,28},{28,24},{1,5},{5... | collective-permute-start | bytes 6291464 | tf_op jit(solution)/shard_map/ppermute | solution.py:575
  19.2 23.1 %collective-permute-start.82 = (bf16[2,256,512]{2,1,0:T(8,128)(2,1)}, bf16[2,256,512]{2,1,0:T(8,128)(2,1)S(1)}, u32[]{:S(2)}, u32[]{:S(2)}) collective-permute-start(bf16[2,256,512]{2,1,0:T(8,128)(2,1)} %get-tuple-element.422.refs_0_), channel_id=1, source_target_pairs={{0,8},{4,12},{8,0},{12,4},{16,24},{20,28},{24,16},{28,20},{1,9},{5... | collective-permute-start | bytes 1572872 | tf_op jit(solution)/shard_map/ppermute | solution.py:603
  22.2 20.1 %collective-permute-start.81 = (bf16[2,256,512]{2,1,0:T(8,128)(2,1)}, bf16[2,256,512]{2,1,0:T(8,128)(2,1)S(1)}, u32[]{:S(2)}, u32[]{:S(2)}) collective-permute-start(bf16[2,256,512]{2,1,0:T(8,128)(2,1)} %get-tuple-element.423), channel_id=1, source_target_pairs={{0,16},{4,20},{8,24},{12,28},{16,0},{20,4},{24,8},{28,12},{1,17},{... | collective-permute-start | bytes 1572872 | tf_op jit(solution)/shard_map/ppermute | solution.py:604
  31.8 35.0 %collective-permute-start.84 = (bf16[2,256,512]{2,1,0:T(8,128)(2,1)}, bf16[2,256,512]{2,1,0:T(8,128)(2,1)}, u32[]{:S(2)}, u32[]{:S(2)}) collective-permute-start(bf16[2,256,512]{2,1,0:T(8,128)(2,1)} %get-tuple-element.425), channel_id=1, source_target_pairs={{0,16},{4,20},{8,24},{12,28},{16,0},{20,4},{24,8},{28,12},{1,17},{... | collective-permute-start | bytes 1572872 | tf_op jit(solution)/shard_map/ppermute | solution.py:604
  32.4 34.4 %collective-permute-start.85 = (bf16[2,256,512]{2,1,0:T(8,128)(2,1)}, bf16[2,256,512]{2,1,0:T(8,128)(2,1)}, u32[]{:S(2)}, u32[]{:S(2)}) collective-permute-start(bf16[2,256,512]{2,1,0:T(8,128)(2,1)} %get-tuple-element.426), channel_id=1, source_target_pairs={{0,8},{4,12},{8,0},{12,4},{16,24},{20,28},{24,16},{28,20},{1,9},{5... | collective-permute-start | bytes 1572872 | tf_op jit(solution)/shard_map/ppermute | solution.py:603
  61.5 39.3 %all-to-all-start = ((f32[32,4,2048]{2,0,1:T(8,128)}), f32[32,4,2048]{2,0,1:T(8,128)}, u32[]{:S(2)}, u32[]{:S(2)}) async-start(f32[32,4,2048]{2,0,1:T(8,128)} %bitcast.39), calls=%async_computation | async-start | bytes 2097152 | tf_op jit(solution)/shard_map/all_to_all | solution.py:510
  71.0 15.0 %collective-permute-start.88 = (bf16[2,256,512]{2,1,0:T(8,128)(2,1)}, bf16[2,256,512]{2,1,0:T(8,128)(2,1)S(1)}, u32[]{:S(2)}, u32[]{:S(2)}) collective-permute-start(bf16[2,256,512]{2,1,0:T(8,128)(2,1)} %get-tuple-element.428), channel_id=1, source_target_pairs={{0,16},{4,20},{8,24},{12,28},{16,0},{20,4},{24,8},{28,12},{1,17},{... | collective-permute-start | bytes 1572872 | tf_op jit(solution)/shard_map/ppermute | solution.py:604
  72.5 15.1 %collective-permute-start.91 = (bf16[2,256,512]{2,1,0:T(8,128)(2,1)}, bf16[2,256,512]{2,1,0:T(8,128)(2,1)}, u32[]{:S(2)}, u32[]{:S(2)}) collective-permute-start(bf16[2,256,512]{2,1,0:T(8,128)(2,1)} %collective-permute-done.84.refs_3_.refs_5_), channel_id=1, source_target_pairs={{0,4},{4,0},{8,12},{12,8},{16,20},{20,16},{24,28},{28,24},{1,5},{5... | collective-permute-start | bytes 1572872 | tf_op jit(solution)/shard_map/ppermute | solution.py:575
  73.0 21.5 %collective-permute-start.101 = (bf16[2,256,512]{2,1,0:T(8,128)(2,1)}, bf16[2,256,512]{2,1,0:T(8,128)(2,1)}, u32[]{:S(2)}, u32[]{:S(2)}) collective-permute-start(bf16[2,256,512]{2,1,0:T(8,128)(2,1)} %get-tuple-element.433), channel_id=1, source_target_pairs={{0,16},{4,20},{8,24},{12,28},{16,0},{20,4},{24,8},{28,12},{1,17},{... | collective-permute-start | bytes 1572872 | tf_op jit(solution)/shard_map/ppermute | solution.py:604
  90.3 16.2 %collective-permute-start.93 = (bf16[2,256,512]{2,1,0:T(8,128)(2,1)}, bf16[2,256,512]{2,1,0:T(8,128)(2,1)}, u32[]{:S(2)}, u32[]{:S(2)}) collective-permute-start(bf16[2,256,512]{2,1,0:T(8,128)(2,1)} %get-tuple-element.430), channel_id=1, source_target_pairs={{0,8},{4,12},{8,0},{12,4},{16,24},{20,28},{24,16},{28,20},{1,9},{5... | collective-permute-start | bytes 1572872 | tf_op jit(solution)/shard_map/ppermute | solution.py:603
  97.1 35.5 %collective-permute-start.113 = (bf16[8,256,512]{2,1,0:T(8,128)(2,1)}, bf16[8,256,512]{2,1,0:T(8,128)(2,1)}, u32[]{:S(2)}, u32[]{:S(2)}) collective-permute-start(bf16[8,256,512]{2,1,0:T(8,128)(2,1)} %write_tokens.6.refs_0_.refs_1_.refs_3_), channel_id=1, source_target_pairs={{0,4},{4,0},{8,12},{12,8},{16,20},{20,16},{24,28},{28,24},{1,5},{5... | collective-permute-start | bytes 6291464 | tf_op jit(solution)/shard_map/ppermute | solution.py:575
  97.1 35.7 %collective-permute-start.116 = (bf16[8,256,512]{2,1,0:T(8,128)(2,1)S(1)}, bf16[8,256,512]{2,1,0:T(8,128)(2,1)}, u32[]{:S(2)}, u32[]{:S(2)}) collective-permute-start(bf16[8,256,512]{2,1,0:T(8,128)(2,1)S(1)} %write_tokens.4.refs_0_.refs_1_.refs_3_.refs_8_), channel_id=1, source_target_pairs={{0,4},{4,0},{8,12},{12,8},{16,20},{20,16},{24,28},{28,24},{1,5},{5... | collective-permute-start | bytes 6291464 | tf_op jit(solution)/shard_map/ppermute | solution.py:575
  100.3 16.3 %collective-permute-start.106 = (bf16[2,256,512]{2,1,0:T(8,128)(2,1)}, bf16[2,256,512]{2,1,0:T(8,128)(2,1)}, u32[]{:S(2)}, u32[]{:S(2)}) collective-permute-start(bf16[2,256,512]{2,1,0:T(8,128)(2,1)} %get-tuple-element.435), channel_id=1, source_target_pairs={{0,8},{4,12},{8,0},{12,4},{16,24},{20,28},{24,16},{28,20},{1,9},{5... | collective-permute-start | bytes 1572872 | tf_op jit(solution)/shard_map/ppermute | solution.py:603
  109.3 17.1 %collective-permute-start.105 = (bf16[2,256,512]{2,1,0:T(8,128)(2,1)}, bf16[2,256,512]{2,1,0:T(8,128)(2,1)}, u32[]{:S(2)}, u32[]{:S(2)}) collective-permute-start(bf16[2,256,512]{2,1,0:T(8,128)(2,1)} %get-tuple-element.434), channel_id=1, source_target_pairs={{0,16},{4,20},{8,24},{12,28},{16,0},{20,4},{24,8},{28,12},{1,17},{... | collective-permute-start | bytes 1572872 | tf_op jit(solution)/shard_map/ppermute | solution.py:604
  132.6 42.1 %collective-permute-start.115 = (bf16[2,256,512]{2,1,0:T(8,128)(2,1)}, bf16[2,256,512]{2,1,0:T(8,128)(2,1)}, u32[]{:S(2)}, u32[]{:S(2)}) collective-permute-start(bf16[2,256,512]{2,1,0:T(8,128)(2,1)} %collective-permute-done.92.refs_7_), channel_id=1, source_target_pairs={{0,4},{4,0},{8,12},{12,8},{16,20},{20,16},{24,28},{28,24},{1,5},{5... | collective-permute-start | bytes 1572872 | tf_op jit(solution)/shard_map/ppermute | solution.py:575
  132.8 34.5 %collective-permute-start.94 = (bf16[2,256,512]{2,1,0:T(8,128)(2,1)}, bf16[2,256,512]{2,1,0:T(8,128)(2,1)S(1)}, u32[]{:S(2)}, u32[]{:S(2)}) collective-permute-start(bf16[2,256,512]{2,1,0:T(8,128)(2,1)} %get-tuple-element.431), channel_id=1, source_target_pairs={{0,8},{4,12},{8,0},{12,4},{16,24},{20,28},{24,16},{28,20},{1,9},{5... | collective-permute-start | bytes 1572872 | tf_op jit(solution)/shard_map/ppermute | solution.py:603
  133.3 34.3 %collective-permute-start.95 = (bf16[2,256,512]{2,1,0:T(8,128)(2,1)}, bf16[2,256,512]{2,1,0:T(8,128)(2,1)S(1)}, u32[]{:S(2)}, u32[]{:S(2)}) collective-permute-start(bf16[2,256,512]{2,1,0:T(8,128)(2,1)} %get-tuple-element.432), channel_id=1, source_target_pairs={{0,16},{4,20},{8,24},{12,28},{16,0},{20,4},{24,8},{28,12},{1,17},{... | collective-permute-start | bytes 1572872 | tf_op jit(solution)/shard_map/ppermute | solution.py:604
  135.8 32.1 %collective-permute-start.107 = (bf16[2,256,512]{2,1,0:T(8,128)(2,1)}, bf16[2,256,512]{2,1,0:T(8,128)(2,1)}, u32[]{:S(2)}, u32[]{:S(2)}) collective-permute-start(bf16[2,256,512]{2,1,0:T(8,128)(2,1)} %get-tuple-element.436), channel_id=1, source_target_pairs={{0,8},{4,12},{8,0},{12,4},{16,24},{20,28},{24,16},{28,20},{1,9},{5... | collective-permute-start | bytes 1572872 | tf_op jit(solution)/shard_map/ppermute | solution.py:603
  136.4 31.7 %collective-permute-start.108 = (bf16[2,256,512]{2,1,0:T(8,128)(2,1)}, bf16[2,256,512]{2,1,0:T(8,128)(2,1)}, u32[]{:S(2)}, u32[]{:S(2)}) collective-permute-start(bf16[2,256,512]{2,1,0:T(8,128)(2,1)} %get-tuple-element.437), channel_id=1, source_target_pairs={{0,16},{4,20},{8,24},{12,28},{16,0},{20,4},{24,8},{28,12},{1,17},{... | collective-permute-start | bytes 1572872 | tf_op jit(solution)/shard_map/ppermute | solution.py:604
  137.8 24.5 %all-to-all-start.1 = ((bf16[8,4,4096]{2,1,0:T(4,128)(2,1)}), bf16[8,4,4096]{2,1,0:T(4,128)(2,1)S(1)}, u32[]{:S(2)}, u32[]{:S(2)}) async-start(bf16[8,4,4096]{2,1,0:T(4,128)(2,1)} %pad_maximum_fusion.1), calls=%async_computation.1 | async-start | bytes 524288 | tf_op jit(solution)/shard_map/all_to_all | solution.py:523
  184.3 15.2 %collective-permute-start = (bf16[2,256,512]{2,1,0:T(8,128)(2,1)}, bf16[2,256,512]{2,1,0:T(8,128)(2,1)}, u32[]{:S(2)}, u32[]{:S(2)}) collective-permute-start(bf16[2,256,512]{2,1,0:T(8,128)(2,1)} %get-tuple-element.267), channel_id=1, source_target_pairs={{0,8},{4,12},{8,0},{12,4},{16,24},{20,28},{24,16},{28,20},{1,9},{5... | collective-permute-start | bytes 1572872 | tf_op jit(solution)/shard_map/cond/branch_1_fun/ppermute | solution.py:603
  185.2 15.1 %collective-permute-start.1 = (bf16[2,256,512]{2,1,0:T(8,128)(2,1)}, bf16[2,256,512]{2,1,0:T(8,128)(2,1)}, u32[]{:S(2)}, u32[]{:S(2)}) collective-permute-start(bf16[2,256,512]{2,1,0:T(8,128)(2,1)} %get-tuple-element.268), channel_id=1, source_target_pairs={{0,16},{4,20},{8,24},{12,28},{16,0},{20,4},{24,8},{28,12},{1,17},{... | collective-permute-start | bytes 1572872 | tf_op jit(solution)/shard_map/cond/branch_1_fun/ppermute | solution.py:604
  187.1 22.8 %collective-permute-start.2 = (bf16[2,256,512]{2,1,0:T(8,128)(2,1)}, bf16[2,256,512]{2,1,0:T(8,128)(2,1)S(1)}, u32[]{:S(2)}, u32[]{:S(2)}) collective-permute-start(bf16[2,256,512]{2,1,0:T(8,128)(2,1)} %get-tuple-element.279), channel_id=1, source_target_pairs={{0,8},{4,12},{8,0},{12,4},{16,24},{20,28},{24,16},{28,20},{1,9},{5... | collective-permute-start | bytes 1572872 | tf_op jit(solution)/shard_map/cond/branch_1_fun/ppermute | solution.py:603
  189.5 20.4 %collective-permute-start.3 = (bf16[2,256,512]{2,1,0:T(8,128)(2,1)}, bf16[2,256,512]{2,1,0:T(8,128)(2,1)S(1)}, u32[]{:S(2)}, u32[]{:S(2)}) collective-permute-start(bf16[2,256,512]{2,1,0:T(8,128)(2,1)} %get-tuple-element.280), channel_id=1, source_target_pairs={{0,16},{4,20},{8,24},{12,28},{16,0},{20,4},{24,8},{28,12},{1,17},{... | collective-permute-start | bytes 1572872 | tf_op jit(solution)/shard_map/cond/branch_1_fun/ppermute | solution.py:604
  (45 other events, 595.5 us)

commit v2 on v1

--- a/solution.py
+++ b/solution.py
@@ -2,6 +2,7 @@
 import itertools
 import math
 import random
+import types
 
 import jax
 import jax.numpy as jnp
@@ -14,10 +15,12 @@
 
 D = 8192
 HEAD_SIZE = 128
+SECTION = "section"
+TENSOR = "tensor"
 PIECES = 4
 STREAMS = 2
 MAX_ROUNDS = 8
-BASE_ROUNDS = 4
+BASE_ROUNDS = 5
 FIELDS = 2 * MAX_ROUNDS + 8 * PIECES
 RING = (0, 1, 3, 2)
 
@@ -208,13 +211,13 @@
             pltpu.SMEM((4,), jnp.int32),
             pltpu.SemaphoreType.DMA,
         ],
-        name="find_route",
     )(place, matching, jnp.asarray(index), jnp.asarray(rows))
 
 
 def write_kernel(
-    rows, first_of, place_ref, lengths_ref, cache_ref, fresh_ref, out_ref, held, wide, sem_in, sem_out
+    rows, first_of, place_ref, lengths_ref, cache_ref, fresh_ref, *refs
 ):
+    out_ref, held, wide, sem_in, sem_out = refs[-5:]
     first = first_of(place_ref[0])
 
     def copy_in(row):
@@ -240,7 +243,7 @@
         copy_out(row).wait()
 
 
-def write_tokens(place, lengths, kv_cache, fresh, rows, first_of):
+def write_tokens(place, lengths, kv_cache, fresh, rows, first_of, after=()):
     smem = pl.BlockSpec(memory_space=pltpu.SMEM)
     shape = (rows,) + kv_cache.shape[2:]
     return pl.pallas_call(
@@ -251,7 +254,8 @@
             smem,
             pl.BlockSpec(memory_space=pl.ANY),
             pl.BlockSpec(memory_space=pltpu.VMEM),
-        ],
+        ]
+        + [pl.BlockSpec(memory_space=pl.ANY)] * len(after),
         out_specs=pl.BlockSpec(memory_space=pl.ANY),
         scratch_shapes=[
             pltpu.VMEM(shape, kv_cache.dtype),
@@ -259,22 +263,19 @@
             pltpu.SemaphoreType.DMA((rows,)),
             pltpu.SemaphoreType.DMA((rows,)),
         ],
-        name="write_tokens",
         cost_estimate=pl.CostEstimate(
             flops=2 * math.prod(shape), bytes_accessed=4 * math.prod(shape), transcendentals=0
         ),
-    )(place, lengths, kv_cache, fresh)
+    )(place, lengths, kv_cache, fresh, *after)
 
 
 def pick_kernel(step, n_near, n_after, ids_ref, *refs):
-    refs = refs[n_after:]
+    outs, sems = refs[-3:-1], refs[-1]
+    refs = refs[n_after:-3]
     near = refs[:n_near]
-    per = refs[0].shape[0] // PIECES
-    passed = (len(refs) - n_near - 6) // 2
-    relays = (refs[n_near : n_near + passed], refs[n_near + passed : n_near + 2 * passed])
-    outs = refs[-6:-4]
-    held = refs[-4:-2]
-    sem_in, sem_out = refs[-2:]
+    passed = (len(refs) - n_near) // 2
+    relays = (refs[n_near : n_near + passed], refs[n_near + passed :])
+    per = outs[0].shape[0]
     for way in range(2):
         wanted = ids_ref[2 * step + way]
         for number, ref in enumerate(near):
@@ -282,49 +283,37 @@
             @pl.when((wanted >= number * PIECES) & (wanted < (number + 1) * PIECES))
             def _(number=number, ref=ref, wanted=wanted, way=way):
                 start = (wanted - number * PIECES) * per
-                pltpu.make_async_copy(ref.at[pl.ds(start, per)], held[way], sem_in.at[way]).start()
+                pltpu.make_async_copy(ref.at[pl.ds(start, per)], outs[way], sems.at[way]).start()
 
         for past, ref in enumerate(relays[way]):
 
             @pl.when(wanted == 2 * PIECES + 2 * past + 1 - way)
             def _(ref=ref, way=way):
-                pltpu.make_async_copy(ref, held[way], sem_in.at[way]).start()
-
-    def copy_out(way):
-        return pltpu.make_async_copy(held[way], outs[way], sem_out.at[way])
+                pltpu.make_async_copy(ref, outs[way], sems.at[way]).start()
 
     for way in range(2):
-        pltpu.make_async_copy(near[0].at[pl.ds(0, per)], held[way], sem_in.at[way]).wait()
-        copy_out(way).start()
-    for way in range(2):
-        copy_out(way).wait()
+        pltpu.make_async_copy(near[0].at[pl.ds(0, per)], outs[way], sems.at[way]).wait()
 
 
 def pick_pieces(ids, step, near, from_x, from_y, after=()):
     shape = (near[0].shape[0] // PIECES,) + near[0].shape[1:]
-    held = pltpu.VMEM(shape, near[0].dtype)
     anywhere = pl.BlockSpec(memory_space=pl.ANY)
     operands = list(after) + list(near) + list(from_y) + list(from_x)
-    one = jax.ShapeDtypeStruct(shape, near[0].dtype)
+    one = pltpu.VMEM(shape, near[0].dtype)
+    vmem = pl.BlockSpec(memory_space=pltpu.VMEM)
     return pl.pallas_call(
         functools.partial(pick_kernel, step, len(near), len(after)),
         out_shape=(one, one),
         in_specs=[pl.BlockSpec(memory_space=pltpu.SMEM)] + [anywhere] * len(operands),
-        out_specs=(anywhere, anywhere),
-        scratch_shapes=[
-            held,
-            held,
-            pltpu.SemaphoreType.DMA((2,)),
-            pltpu.SemaphoreType.DMA((2,)),
-        ],
-        name="pick_pieces",
+        out_specs=(vmem, vmem),
+        scratch_shapes=[pltpu.SemaphoreType.DMA((2,))],
         cost_estimate=pl.CostEstimate(
             flops=2 * math.prod(shape), bytes_accessed=8 * math.prod(shape), transcendentals=0
         ),
     )(ids, *operands)
 
 
-def place_kernel(lo, hi, per, layout, place_ref, ids_ref, *refs):
+def place_kernel(lo, hi, per, near_at, far_at, place_ref, ids_ref, *refs):
     out_ref, held, sem_in, sem_out = refs[-4:]
     core = place_ref[0] % 2
     blocks = [
@@ -345,13 +334,13 @@
             if lo < 2 * PIECES:
 
                 @pl.when((wanted >= number * PIECES) & (wanted < (number + 1) * PIECES))
-                def _(ref=refs[layout["near"][side][number][stream]]):
+                def _(ref=refs[near_at[side][number][stream]]):
                     start = (wanted - number * PIECES) * per
                     pltpu.make_async_copy(
                         ref.at[pl.ds(start, per)], held.at[at], sem_in.at[at]
                     ).start()
 
-        for slot, position in layout["far"][side][stream].items():
+        for slot, position in far_at[side][stream].items():
             if lo <= slot < hi:
 
                 @pl.when(wanted == slot)
@@ -383,7 +372,8 @@
 
 def place_pieces(place, ids, lo, hi, near, far, result, out_shape, after=()):
     operands = []
-    layout = {"near": [[[0, 0] for _ in range(2)] for _ in range(2)], "far": [[{}, {}], [{}, {}]]}
+    near_at = [[[0, 0] for _ in range(2)] for _ in range(2)]
+    far_at = [[{}, {}], [{}, {}]]
 
     def add(array):
         operands.append(array)
@@ -393,10 +383,10 @@
         for stream in range(STREAMS):
             if lo < 2 * PIECES:
                 for owner in range(2):
-                    layout["near"][side][owner][stream] = add(near[side][owner][stream])
+                    near_at[side][owner][stream] = add(near[side][owner][stream])
             for slot, array in far[side][stream].items():
                 if lo <= slot < hi:
-                    layout["far"][side][stream][slot] = add(array)
+                    far_at[side][stream][slot] = add(array)
     per = out_shape.shape[1] // (2 * STREAMS * PIECES)
     smem = pl.BlockSpec(memory_space=pltpu.SMEM)
     anywhere = pl.BlockSpec(memory_space=pl.ANY)
@@ -407,7 +397,7 @@
         operands.append(result)
     count = 2 * STREAMS * PIECES
     return pl.pallas_call(
-        functools.partial(place_kernel, lo, hi, per, layout),
+        functools.partial(place_kernel, lo, hi, per, near_at, far_at),
         out_shape=out_shape,
         in_specs=[smem, smem] + [anywhere] * len(operands),
         out_specs=anywhere,
@@ -417,7 +407,6 @@
             pltpu.SemaphoreType.DMA((count,)),
         ],
         input_output_aliases=aliases,
-        name="place_pieces",
         cost_estimate=pl.CostEstimate(
             flops=math.prod(out_shape.shape),
             bytes_accessed=2 * math.prod(out_shape.shape),
@@ -482,13 +471,77 @@
             + [pl.BlockSpec(memory_space=pl.ANY)] * len(after),
             out_specs=pl.BlockSpec((block, per_key, HEAD_SIZE), lambda i, _: (i, 0, 0)),
         ),
-        name="attend",
         cost_estimate=pl.CostEstimate(
             flops=30 * work, bytes_accessed=rows * slots * 4 * HEAD_SIZE, transcendentals=0
         ),
     )(lengths, queries, kv_cache, fresh, *after)
 
 
+def add_kernel(parts_ref, residual_ref, stream_ref, squares_ref):
+    total = residual_ref[0].astype(jnp.float32)
+    added = parts_ref[0]
+    for part in range(1, parts_ref.shape[0]):
+        added = added + parts_ref[part]
+    total = total + added
+    stream_ref[...] = total
+    squares = jnp.sum(total * total, axis=-1, keepdims=True)
+    squares_ref[...] = jnp.broadcast_to(squares, squares_ref.shape)
+
+
+def add_parts_kernel(parts, residual):
+    rows, width = residual.shape[1:]
+    return pl.pallas_call(
+        add_kernel,
+        out_shape=(
+            jax.ShapeDtypeStruct((rows, width), jnp.float32),
+            jax.ShapeDtypeStruct((rows, 128), jnp.float32),
+        ),
+        cost_estimate=pl.CostEstimate(
+            flops=8 * parts.size, bytes_accessed=4 * parts.size, transcendentals=0
+        ),
+    )(parts, residual)
+
+
+def norm_kernel(groups, stream_ref, gain_ref, *refs):
+    both_ref = refs[-1]
+    stream = stream_ref[...]
+    squares = refs[0][:, :1]
+    for ref in refs[1:-1]:
+        squares = squares + ref[:, :1]
+    normed = stream * lax.rsqrt(squares / D + 1e-05) * gain_ref[...].astype(jnp.float32)
+    per = stream.shape[0] // groups
+    for group in range(groups):
+        chunk = slice(group * per, (group + 1) * per)
+        pair = jnp.concatenate([stream[chunk], normed[chunk]], axis=0)
+        both_ref[group] = pair.astype(both_ref.dtype)
+
+
+def norm_both(groups, stream, norm_gain, squares):
+    rows, width = stream.shape
+    return pl.pallas_call(
+        functools.partial(norm_kernel, groups),
+        out_shape=jax.ShapeDtypeStruct((groups, 2 * rows // groups, width), jnp.bfloat16),
+        cost_estimate=pl.CostEstimate(
+            flops=60 * stream.size, bytes_accessed=8 * stream.size, transcendentals=0
+        ),
+    )(stream, norm_gain, *squares)
+
+
+def part_kernel(landed_ref, stream_ref, normed_ref):
+    groups, double = landed_ref.shape[:2]
+    per = double // 2
+    landed = landed_ref[...].astype(jnp.float32)
+    for way, ref in enumerate((stream_ref, normed_ref)):
+        chunks = [landed[group, way * per : (way + 1) * per] for group in range(groups)]
+        ref[0] = jnp.concatenate(chunks, axis=0).astype(ref.dtype)
+
+
+def part_both(landed):
+    groups, double, width = landed.shape
+    one = jax.ShapeDtypeStruct((1, groups * double // 2, width), landed.dtype)
+    return pl.pallas_call(part_kernel, out_shape=(one, one))(landed)
+
+
 def shift_pairs(size, shift):
     return [(at, (at + shift) % size) for at in range(size)]
 
@@ -498,16 +551,16 @@
 
 
 def sum_over_tensor(value):
-    size = lax.axis_size("tensor")
+    size = lax.axis_size(TENSOR)
     total = value
     for shift in range(1, size):
-        total = total + lax.ppermute(value, "tensor", shift_pairs(size, shift))
+        total = total + lax.ppermute(value, TENSOR, shift_pairs(size, shift))
     return total
 
 
 def scatter_sum(partial_value):
-    size = lax.axis_size("tensor")
-    parts = lax.all_to_all(partial_value, "tensor", split_axis=1, concat_axis=0, tiled=True)
+    size = lax.axis_size(TENSOR)
+    parts = lax.all_to_all(partial_value, TENSOR, split_axis=1, concat_axis=0, tiled=True)
     return jnp.sum(parts.reshape((size,) + (partial_value.shape[0], -1)), axis=0)
 
 
@@ -518,14 +571,14 @@
 
 
 def spread_rows(matching, value):
-    groups = lax.axis_size("section")
+    groups = lax.axis_size(SECTION)
     folded = value.reshape((groups, value.shape[0] // groups) + value.shape[1:])
-    spread = lax.all_to_all(folded, "section", split_axis=0, concat_axis=0, tiled=True)
+    spread = lax.all_to_all(folded, SECTION, split_axis=0, concat_axis=0, tiled=True)
     return jnp.take(spread, matching, axis=0, mode="clip")
 
 
 def gather_rows(chosen, shape):
-    landed = lax.all_to_all(chosen, "section", split_axis=0, concat_axis=0, tiled=True)
+    landed = lax.all_to_all(chosen, SECTION, split_axis=0, concat_axis=0, tiled=True)
     return landed.reshape(shape)
 
 
@@ -536,7 +589,7 @@
 def on_any_section(
     matching, lengths, queries, kv_cache, incoming_key_value, residual, out_weight, norm_gain
 ):
-    place = lax.axis_index("section").astype(jnp.int32).reshape(1)
+    place = lax.axis_index(SECTION).astype(jnp.int32).reshape(1)
     rows = kv_cache.shape[1]
     updated = write_tokens(
         place, lengths, kv_cache, incoming_key_value, rows, lambda _: 0
@@ -563,8 +616,8 @@
 def on_four_chips(
     matching, lengths, queries, kv_cache, incoming_key_value, residual, out_weight, norm_gain
 ):
-    place = lax.axis_index("section").astype(jnp.int32).reshape(1)
-    sections = lax.axis_size("section")
+    place = lax.axis_index(SECTION).astype(jnp.int32).reshape(1)
+    sections = lax.axis_size(SECTION)
     across_core, across_x, across_y = (flip_pairs(sections, mask) for mask in (1, 2, 4))
     rows = kv_cache.shape[1]
     kv_heads = kv_cache.shape[3] // (2 * HEAD_SIZE)
@@ -572,25 +625,26 @@
     part = rows // (2 * STREAMS)
 
     def swap(array):
-        return lax.ppermute(array, "section", across_core)
+        return lax.ppermute(array, SECTION, across_core)
 
     lent, kept, got = [], [], []
-    for stream in range(STREAMS):
+
+    def share(stream, after=()):
         lent.append(
             write_tokens(
                 place, lengths, kv_cache, fresh, part,
-                lambda p, s=stream: (1 - p % 2) * (rows // 2) + s * part,
+                lambda p: (1 - p % 2) * (rows // 2) + stream * part, after,
             )
         )
         got.append(swap(lent[-1]))
-    ids = find_route(place, matching)
-    for stream in range(STREAMS):
         kept.append(
             write_tokens(
                 place, lengths, kv_cache, fresh, part,
-                lambda p, s=stream: p % 2 * (rows // 2) + s * part,
+                lambda p: p % 2 * (rows // 2) + stream * part, [lent[-1]],
             )
         )
+
+    ids = find_route(place, matching)
 
     from_x = [[] for _ in range(STREAMS)]
     from_y = [[] for _ in range(STREAMS)]
@@ -600,8 +654,8 @@
         out_x, out_y = pick_pieces(
             ids, step, (kept[stream], got[stream]), from_x[stream], from_y[stream], after
         )
-        landed_x = lax.ppermute(out_x, "section", across_x)
-        landed_y = lax.ppermute(out_y, "section", across_y)
+        landed_x = lax.ppermute(out_x, SECTION, across_x)
+        landed_y = lax.ppermute(out_y, SECTION, across_y)
         return ((landed_x, landed_y), out_x)
 
     def receive(step, stream, landed, from_x, from_y, far):
@@ -613,62 +667,84 @@
 
     split_queries = queries.reshape(rows, -1, HEAD_SIZE)
     depth = out_weight.shape[1] // kv_heads
-    work = {}
+    work = types.SimpleNamespace(sent=None)
 
     def attend_head(head):
-        work["attended"] = attend(
-            head, lengths, split_queries, kv_cache, incoming_key_value, [work["sent"]]
-        )
-        return [work["attended"]]
+        work.attended = attend(
+            head, lengths, split_queries, kv_cache, incoming_key_value, [work.sent]
+        )
+        return [work.attended]
 
     def project_head(head):
         product = jnp.dot(
-            work["attended"].reshape(rows, -1),
+            work.attended.reshape(rows, -1),
             out_weight[0, head * depth : (head + 1) * depth],
             preferred_element_type=jnp.float32,
         )
-        work["partial"] = product if head == 0 else work["partial"] + product
-        return [work["partial"]]
+        work.partial = product if head == 0 else work.partial + product
+        return [work.partial]
 
     def add_parts():
-        work["stream"] = residual[0].astype(jnp.float32) + scatter_sum(work["partial"])
-        return [work["stream"]]
+        parts = lax.all_to_all(
+            work.partial, TENSOR, split_axis=1, concat_axis=0, tiled=True
+        )
+        parts = parts.reshape(lax.axis_size(TENSOR), rows, -1)
+        work.stream, squares = add_parts_kernel(parts, residual)
+        tensors = lax.axis_size(TENSOR)
+        work.squares = [squares] + [
+            lax.ppermute(squares, TENSOR, shift_pairs(tensors, shift))
+            for shift in range(1, tensors)
+        ]
+        return [work.stream]
 
     def norm_stream():
-        work["both"] = norm_rows(work["stream"], norm_gain)
-        return [work["both"]]
-
-    def spread_both():
-        work["chosen"] = spread_rows(matching, work["both"])
-        return [work["chosen"]]
-
-    def gather_both():
-        work["moved"] = gather_rows(work["chosen"], work["both"].shape)
-        return [work["moved"]]
+        work.both = norm_both(sections, work.stream, norm_gain, work.squares)
+        return [work.both]
+
+    def move_both():
+        spread = lax.all_to_all(work.both, SECTION, split_axis=0, concat_axis=0, tiled=True)
+        chosen = jnp.take(spread, matching, axis=0, mode="clip")
+        work.landed = lax.all_to_all(
+            chosen, SECTION, split_axis=0, concat_axis=0, tiled=True
+        )
+        return [chosen]
+
+    def split_both():
+        work.outs = part_both(work.landed)
+        return [work.sent]
 
     chores = []
     for head in range(kv_heads):
         chores += [functools.partial(attend_head, head), functools.partial(project_head, head)]
-    chores += [add_parts, norm_stream, spread_both, gather_both]
+    out_shape = jax.ShapeDtypeStruct(kv_cache.shape, kv_cache.dtype)
+    early = 2 * PIECES + 4
+
+    def place_early():
+        lent_back = [swap(array) for array in kept]
+        near = [[kept, got], [lent, lent_back]]
+        work.result = place_pieces(place, ids, 0, early, near, far, None, out_shape, [work.sent])
+        return add_parts()
+
+    chores += [None, place_early, norm_stream, move_both, split_both]
     after = []
     for step in range(BASE_ROUNDS):
         for stream in range(STREAMS):
             settled = [far[1][stream][s] for s in far[1][stream] if s < 2 * PIECES + 2 * step - 2]
-            landed, work["sent"] = send(
+            if step == 0:
+                share(stream, [work.sent] if stream else [])
+            landed, work.sent = send(
                 step, stream, from_x, from_y, kept, got, ids, after + settled[-2:]
             )
             receive(step, stream, landed, from_x, from_y, far)
-            after = []
-            if step + stream > 0 and chores:
-                after = chores.pop(0)()
-    for chore in chores:
+            chore = chores.pop(0) if step + stream > 0 and chores else None
+            after = chore() if chore else []
+    for chore in filter(None, chores):
         after = chore()
-    lent_back = [swap(array) for array in kept]
-    near = [[kept, got], [lent, lent_back]]
-    both = work["moved"]
-    out_shape = jax.ShapeDtypeStruct(kv_cache.shape, kv_cache.dtype)
+    stream_out, normed_out = work.outs
     ready = 2 * PIECES + 2 * (BASE_ROUNDS - 1)
-    result = place_pieces(place, ids, 0, ready, near, far, None, out_shape, after)
+    result = place_pieces(
+        place, ids, early, ready, None, far, work.result, out_shape, after
+    )
 
     def finish(extra, place, ids, kept, got, from_x, from_y, far, result):
         from_x, from_y = [list(a) for a in from_x], [list(a) for a in from_y]
@@ -691,29 +767,28 @@
         [functools.partial(finish, extra) for extra in range(MAX_ROUNDS - BASE_ROUNDS + 1)],
         place, ids, kept, got, from_x, from_y, late, result,
     )
-    width = both.shape[1] // 2
-    return (cache_out, both[None, :, :width], both[None, :, width:])
+    return (cache_out, stream_out, normed_out)
 
 
 def solution(mesh):
-    four_chips = mesh.shape["section"] == 8
+    four_chips = mesh.shape[SECTION] == 8
     return jax.shard_map(
         on_four_chips if four_chips else on_any_section,
         mesh=mesh,
         in_specs=(
             P(),
             P(),
-            P("section", None, "tensor"),
-            P("section", None, None, "tensor"),
-            P("section", None, "tensor"),
-            P("section", None, "tensor"),
-            P("section", "tensor", None),
-            P("section", "tensor"),
+            P(SECTION, None, TENSOR),
+            P(SECTION, None, None, TENSOR),
+            P(SECTION, None, TENSOR),
+            P(SECTION, None, TENSOR),
+            P(SECTION, TENSOR, None),
+            P(SECTION, TENSOR),
         ),
         out_specs=(
-            P("section", None, None, "tensor"),
-            P("section", None, "tensor"),
-            P("section", None, "tensor"),
+            P(SECTION, None, None, TENSOR),
+            P(SECTION, None, TENSOR),
+            P(SECTION, None, TENSOR),
         ),
         check_vma=False,
     )

time: 218 us -> 212 us (0.972)
  waiting for transfers between devices: 68.6 us -> 82.8 us
  other arithmetic: 9.19 us -> 0.01 us
  local copies, waits for them, and re-layouts: 11.5 us -> 6.02 us
  Pallas kernels: 61.2 us -> 58.9 us
    ppermute x47, waiting for transfers between devices: 43.5 us -> 77.6 us  [the longest x10 52.9 us: send(): landed_x = lax.ppermute(out_x, SECTION, across_x)]
    all_to_all x3, waiting for transfers between devices: 25.1 us -> 5.27 us  [the longest x1 3.59 us: move_both(): lax.all_to_all(work.both, SECTION, split_axis=0, concat_axis=0, tiled=True)]
    pallas_call x10, Pallas kernels: 25.3 us -> 17.6 us  [pick_pieces(): pl.pallas_call(functools.partial(pick_kernel, step, len(near), len(after)...]
    pallas_call x3 -> x6, Pallas kernels: 10.3 us -> 14.9 us  [the longest x3 9.16 us: place_pieces(): pl.pallas_call(functools.partial(place_kernel, lo, hi, per, near_at, far_...]
    convert_element_type x3 -> x0, other arithmetic: 3.78 us -> none  [the longest x2 2.74 us: norm_rows(): stream.astype(jnp.bfloat16)]
  transfers between devices with their start and end apart: 50 -> 50, of which waited for: 13 -> 17; matrix products, arithmetic and copies ran while one was open for 17% -> 11% of each run, Pallas kernels for 25% -> 23%
where the time goes in v2:
time: 212 us; the launch traced here: 211 us
  waiting for transfers between devices  82.8 us (39%)
  Pallas kernels  58.9 us (28%)
  starting transfers between devices  42.6 us (20%)
  matrix products  18.8 us (9%)
  local copies, waits for them, and re-layouts  6.02 us (3%)
    ppermute x10, waiting for transfers between devices, send(): landed_x = lax.ppermute(out_x, SECTION, across_x)  52.9 us
    ppermute x10, waiting for transfers between devices, send(): landed_y = lax.ppermute(out_y, SECTION, across_y)  22.9 us
    dot_general x2, matrix products, project_head(): jnp.dot(work.attended.reshape(rows, -1), out_weight[0, head * depth:(head...  18.8 us
    pallas_call x10, Pallas kernels, pick_pieces(): pl.pallas_call(functools.partial(pick_kernel, step, len(near), len(after)...  17.6 us
    pallas_call x4, Pallas kernels, write_tokens(): pl.pallas_call(functools.partial(write_kernel, rows, first_of), out_shape...  13 us
    pallas_call x2, Pallas kernels, attend(): pl.pallas_call(functools.partial(attend_kernel, block), out_shape=jax.Sha...  11.1 us
    ppermute x10, starting transfers between devices, send(): landed_y = lax.ppermute(out_y, SECTION, across_y)  10.7 us
    ppermute x10, starting transfers between devices, send(): landed_x = lax.ppermute(out_x, SECTION, across_x)  10.6 us
  transfers between devices with their start and end apart: 50, of which 17 were waited for; matrix products, arithmetic and copies ran while one was open for 11% of the time, Pallas kernels for 23%

profile of v2, /device:TPU:0, one launch (start us, length us, event | category | flops | bytes accessed | tf_op | source)
XLA Modules:
  0.0 211.1 jit_solution(6436454731997441874)
XLA Ops:
  0.6 3.3 %shard_map.122.refs_0_.refs_12_ = bf16[8,256,512]{2,1,0:T(8,128)(2,1)} custom-call(s32[1]{0:T(128)} %bitcast.place_ref, s32[32]{0:T(128)} %lengths_ref.11, bf16[1,32,256,512]{3,2,1,0:T(8,128)(2,1)} %cache_ref.11, bf16[1,32,512]{2,1,0:T(8,128)(2,1)} %fresh_ref.11), custom_call_target="tpu_custom_call" | custom-call | flops 2097152 | bytes 4194304 | tf_op jit(solution)/shard_map/pallas_call | solution.py:249
  6.9 3.2 %shard_map.123.refs_0_.refs_1_.refs_3_.refs_2_ = bf16[8,256,512]{2,1,0:T(8,128)(2,1)} custom-call(s32[1]{0:T(128)} %bitcast.place_ref, s32[32]{0:T(128)} %lengths_ref.11, bf16[1,32,256,512]{3,2,1,0:T(8,128)(2,1)} %cache_ref.11, bf16[1,32,512]{2,1,0:T(8,128)(2,1)} %fresh_ref.11, bf16[8,256,512]{2,1,0:T(8,128)(2,1)} %shard_map.122.refs_0_.refs_12_), custom_call_target="tpu_custom_call" | custom-call | flops 2097152 | bytes 4194304 | tf_op jit(solution)/shard_map/pallas_call | solution.py:249
  12.7 3.2 %shard_map.125.refs_0_.refs_18_ = bf16[8,256,512]{2,1,0:T(8,128)(2,1)} custom-call(s32[1]{0:T(128)} %bitcast.place_ref, s32[32]{0:T(128)} %lengths_ref.11, bf16[1,32,256,512]{3,2,1,0:T(8,128)(2,1)} %cache_ref.11, bf16[1,32,512]{2,1,0:T(8,128)(2,1)} %fresh_ref.11, bf16[2,256,512]{2,1,0:T(8,128)(2,1)} %copy-done.5), custom_call_target="tpu_custom_call" | custom-call | flops 2097152 | bytes 4194304 | tf_op jit(solution)/shard_map/pallas_call | solution.py:249
  16.0 3.0 %collective-permute-start.55 = (bf16[2,256,512]{2,1,0:T(8,128)(2,1)S(1)}, bf16[2,256,512]{2,1,0:T(8,128)(2,1)}, u32[]{:S(2)}, u32[]{:S(2)}) collective-permute-start(bf16[2,256,512]{2,1,0:T(8,128)(2,1)S(1)} %copy-done.6), channel_id=1, source_target_pairs={{0,8},{4,12},{8,0},{12,4},{16,24},{20,28},{24,16},{28,20},{1,9},{5... | collective-permute-start | bytes 1572872 | tf_op jit(solution)/shard_map/ppermute | solution.py:657
  20.5 3.2 %shard_map.126.refs_0_.refs_1_.refs_3_.refs_6_ = bf16[8,256,512]{2,1,0:T(8,128)(2,1)} custom-call(s32[1]{0:T(128)} %bitcast.place_ref, s32[32]{0:T(128)} %lengths_ref.11, bf16[1,32,256,512]{3,2,1,0:T(8,128)(2,1)} %cache_ref.11, bf16[1,32,512]{2,1,0:T(8,128)(2,1)} %fresh_ref.11, bf16[8,256,512]{2,1,0:T(8,128)(2,1)} %shard_map.125.refs_0_.refs_18_), custom_call_target="tpu_custom_call" | custom-call | flops 2097152 | bytes 4194304 | tf_op jit(solution)/shard_map/pallas_call | solution.py:249
  26.7 4.5 %collective-permute-done.55.refs_4_.refs_7_.refs_9_.refs_2_ = bf16[2,256,512]{2,1,0:T(8,128)(2,1)} collective-permute-done((bf16[2,256,512]{2,1,0:T(8,128)(2,1)S(1)}, bf16[2,256,512]{2,1,0:T(8,128)(2,1)}, u32[]{:S(2)}, u32[]{:S(2)}) %collective-permute-start.55) | collective-permute-done | bytes 524320 | tf_op jit(solution)/shard_map/ppermute | solution.py:657
  33.9 5.5 %shard_map.128.refs_0_ = bf16[32,8,128]{2,1,0:T(8,128)(2,1)} custom-call(s32[32]{0:T(128)} %lengths_ref.11, bf16[32,16,128]{2,1,0:T(8,128)(2,1)} %bitcast.28, bf16[1,32,256,512]{3,2,1,0:T(8,128)(2,1)} %cache_ref.11, bf16[1,32,512]{2,1,0:T(8,128)(2,1)} %fresh_ref.11, bf16[2,256,512]{2,1,0:T(8,128)(2,1)} %copy-done.4), custom_call_target="tpu_custom_call" | custom-call | flops 251658240 | bytes 4194304 | tf_op jit(solution)/shard_map/pallas_call | solution.py:460
  44.7 9.8 %fusion.2.refs_0_ = f32[32,8192]{1,0:T(8,128)} fusion(bf16[1,2048,8192]{2,1,0:T(8,128)(2,1)} %param.20, bf16[4,8,8,128]{3,2,1,0:T(8,128)(2,1)} %bitcast.31), kind=kOutput, calls=%fused_computation.3 | convolution fusion | flops 536870912 | bytes 17891328 | tf_op jit(solution)/shard_map/dot_general | solution.py:679
  57.1 5.6 %shard_map.130.refs_0_ = bf16[32,8,128]{2,1,0:T(8,128)(2,1)} custom-call(s32[32]{0:T(128)} %lengths_ref.11, bf16[32,16,128]{2,1,0:T(8,128)(2,1)} %bitcast.29, bf16[1,32,256,512]{3,2,1,0:T(8,128)(2,1)} %cache_ref.11, bf16[1,32,512]{2,1,0:T(8,128)(2,1)} %fresh_ref.11, bf16[2,256,512]{2,1,0:T(8,128)(2,1)} %copy-done.2), custom_call_target="tpu_custom_call" | custom-call | flops 251658240 | bytes 4194304 | tf_op jit(solution)/shard_map/pallas_call | solution.py:460
  68.6 10.7 %collective-permute-done.61.refs_9_.refs_11_.refs_0_ = bf16[2,256,512]{2,1,0:T(8,128)(2,1)S(1)} collective-permute-done((bf16[2,256,512]{2,1,0:T(8,128)(2,1)S(1)}, bf16[2,256,512]{2,1,0:T(8,128)(2,1)S(1)}, u32[]{:S(2)}, u32[]{:S(2)}) %collective-permute-start.61) | collective-permute-done | bytes 524320 | tf_op jit(solution)/shard_map/ppermute | solution.py:657
  79.4 10.0 %collective-permute-done.74.refs_8_.refs_9_.refs_10_ = bf16[2,256,512]{2,1,0:T(8,128)(2,1)} collective-permute-done((bf16[2,256,512]{2,1,0:T(8,128)(2,1)S(1)}, bf16[2,256,512]{2,1,0:T(8,128)(2,1)}, u32[]{:S(2)}, u32[]{:S(2)}) %collective-permute-start.74) | collective-permute-done | bytes 524320 | tf_op jit(solution)/shard_map/ppermute | solution.py:657
  89.4 9.1 %fusion.6.refs_0_ = f32[32,8192]{1,0:T(8,128)S(1)} fusion(f32[32,8192]{1,0:T(8,128)} %fusion.2.refs_0_, bf16[1,2048,8192]{2,1,0:T(8,128)(2,1)} %param.20, bf16[4,8,8,128]{3,2,1,0:T(8,128)(2,1)} %bitcast.30), kind=kOutput, calls=%fused_computation.7 | convolution fusion | flops 537133056 | bytes 18939904 | tf_op jit(solution)/shard_map/dot_general | solution.py:679
  99.6 4.9 %all-to-all-start = ((f32[32,4,2048]{2,0,1:T(8,128)}), f32[32,4,2048]{2,0,1:T(8,128)}, u32[]{:S(2)}, u32[]{:S(2)}) async-start(f32[32,4,2048]{2,0,1:T(8,128)} %bitcast.27), calls=%async_computation | async-start | bytes 2097152 | tf_op jit(solution)/shard_map/all_to_all | solution.py:688
  112.0 10.0 %collective-permute-done.75.refs_10_.refs_11_.refs_4_ = bf16[2,256,512]{2,1,0:T(8,128)(2,1)} collective-permute-done((bf16[2,256,512]{2,1,0:T(8,128)(2,1)S(1)}, bf16[2,256,512]{2,1,0:T(8,128)(2,1)}, u32[]{:S(2)}, u32[]{:S(2)}) %collective-permute-start.75) | collective-permute-done | bytes 524320 | tf_op jit(solution)/shard_map/ppermute | solution.py:657
  122.5 10.0 %collective-permute-done.68.refs_12_.refs_2_ = bf16[2,256,512]{2,1,0:T(8,128)(2,1)} collective-permute-done((bf16[2,256,512]{2,1,0:T(8,128)(2,1)S(1)}, bf16[2,256,512]{2,1,0:T(8,128)(2,1)}, u32[]{:S(2)}, u32[]{:S(2)}) %collective-permute-start.68) | collective-permute-done | bytes 524320 | tf_op jit(solution)/shard_map/ppermute | solution.py:657
  149.0 4.1 %collective-permute-done.81.refs_8_.refs_7_ = bf16[2,256,512]{2,1,0:T(8,128)(2,1)S(1)} collective-permute-done((bf16[2,256,512]{2,1,0:T(8,128)(2,1)S(1)}, bf16[2,256,512]{2,1,0:T(8,128)(2,1)S(1)}, u32[]{:S(2)}, u32[]{:S(2)}) %collective-permute-start.81) | collective-permute-done | bytes 524320 | tf_op jit(solution)/shard_map/ppermute | solution.py:658
  155.1 3.4 %all-to-all-start.1 = ((bf16[8,8,2048]{2,1,0:T(8,128)(2,1)}), bf16[8,8,2048]{2,1,0:T(8,128)(2,1)S(1)}, u32[]{:S(2)}, u32[]{:S(2)}) async-start(bf16[8,8,2048]{2,1,0:T(8,128)(2,1)} %shard_map.132.refs_0_), calls=%async_computation.1 | async-start | bytes 524288 | tf_op jit(solution)/shard_map/all_to_all | solution.py:705
  162.3 3.6 %all-to-all-done.1 = bf16[8,8,2048]{2,1,0:T(8,128)(2,1)S(1)} async-done(((bf16[8,8,2048]{2,1,0:T(8,128)(2,1)}), bf16[8,8,2048]{2,1,0:T(8,128)(2,1)S(1)}, u32[]{:S(2)}, u32[]{:S(2)}) %all-to-all-start.1) | async-done | bytes 262176 | tf_op jit(solution)/shard_map/all_to_all | solution.py:705
  171.3 5.1 %collective-permute-done.69 = bf16[2,256,512]{2,1,0:T(8,128)(2,1)} collective-permute-done((bf16[2,256,512]{2,1,0:T(8,128)(2,1)S(1)}, bf16[2,256,512]{2,1,0:T(8,128)(2,1)}, u32[]{:S(2)}, u32[]{:S(2)}) %collective-permute-start.69) | collective-permute-done | bytes 524320 | tf_op jit(solution)/shard_map/ppermute | solution.py:657
  176.4 7.6 %collective-permute-done.70 = bf16[2,256,512]{2,1,0:T(8,128)(2,1)} collective-permute-done((bf16[2,256,512]{2,1,0:T(8,128)(2,1)S(1)}, bf16[2,256,512]{2,1,0:T(8,128)(2,1)}, u32[]{:S(2)}, u32[]{:S(2)}) %collective-permute-start.70) | collective-permute-done | bytes 524320 | tf_op jit(solution)/shard_map/ppermute | solution.py:658
  187.0 5.9 %collective-permute-done.84 = bf16[2,256,512]{2,1,0:T(8,128)(2,1)} collective-permute-done((bf16[2,256,512]{2,1,0:T(8,128)(2,1)S(1)}, bf16[2,256,512]{2,1,0:T(8,128)(2,1)}, u32[]{:S(2)}, u32[]{:S(2)}) %collective-permute-start.84) | collective-permute-done | bytes 524320 | tf_op jit(solution)/shard_map/ppermute | solution.py:658
  192.9 3.4 %all-to-all-start.2 = ((bf16[8,8,2048]{2,1,0:T(8,128)(2,1)}), bf16[8,8,2048]{2,1,0:T(8,128)(2,1)S(1)}, u32[]{:S(2)}, u32[]{:S(2)}) async-start(bf16[8,8,2048]{2,1,0:T(8,128)(2,1)} %gather_fusion), calls=%async_computation.2 | async-start | bytes 524288 | tf_op jit(solution)/shard_map/all_to_all | solution.py:707
  197.6 3.9 %shard_map.140.refs_17_ = bf16[1,32,256,512]{3,2,1,0:T(8,128)(2,1)} custom-call(s32[1]{0:T(128)} %bitcast.place_ref, s32[32]{0:T(128)S(1)} %shard_map.121.ids_ref, bf16[8,256,512]{2,1,0:T(8,128)(2,1)} %shard_map.123.refs_0_.refs_1_.refs_3_.refs_2_, bf16[8,256,512]{2,1,0:T(8,128)(2,1)} %collective-permute-done.48.refs_1_.refs_2_.refs_4_.refs_3_, ...), custom_call_target="tpu_custom_call" | custom-call | flops 4194304 | bytes 8388608 | tf_op jit(solution)/shard_map/pallas_call | solution.py:399
  205.6 4.3 %shard_map.141 = bf16[1,32,256,512]{3,2,1,0:T(8,128)(2,1)} custom-call(s32[1]{0:T(128)} %bitcast.place_ref, s32[32]{0:T(128)S(1)} %shard_map.121.ids_ref, bf16[2,256,512]{2,1,0:T(8,128)(2,1)} %copy-done.19, bf16[2,256,512]{2,1,0:T(8,128)(2,1)} %collective-permute-done.63.refs_6_.refs_7_.refs_1_, ...), custom_call_target="tpu_custom_call", output_to_operand_aliasing={{}: (19, {})} | custom-call | flops 4194304 | bytes 8388608 | tf_op jit(solution)/shard_map/pallas_call | solution.py:399
  (151 shorter events, 72.8 us)
Async XLA Ops:
  25.5 18.3 %collective-permute-start.50 = (bf16[2,256,512]{2,1,0:T(8,128)(2,1)S(1)}, bf16[2,256,512]{2,1,0:T(8,128)(2,1)S(1)}, u32[]{:S(2)}, u32[]{:S(2)}) collective-permute-start(bf16[2,256,512]{2,1,0:T(8,128)(2,1)S(1)} %get-tuple-element.370), channel_id=1, source_target_pairs={{0,16},{4,20},{8,24},{12,28},{16,0},{20,4},{24,8},{28,12},{1,17},{... | collective-permute-start | bytes 1572872 | tf_op jit(solution)/shard_map/ppermute | solution.py:658
  31.2 31.5 %collective-permute-start.56 = (bf16[2,256,512]{2,1,0:T(8,128)(2,1)}, bf16[2,256,512]{2,1,0:T(8,128)(2,1)}, u32[]{:S(2)}, u32[]{:S(2)}) collective-permute-start(bf16[2,256,512]{2,1,0:T(8,128)(2,1)} %collective-permute-done.55.refs_4_.refs_7_.refs_9_.refs_2_), channel_id=1, source_target_pairs={{0,4},{4,0},{8,12},{12,8},{16,20},{20,16},{24,28},{28,24},{1,5},{5... | collective-permute-start | bytes 1572872 | tf_op jit(solution)/shard_map/ppermute | solution.py:628
  33.8 28.9 %collective-permute-start.58 = (bf16[2,256,512]{2,1,0:T(8,128)(2,1)}, bf16[2,256,512]{2,1,0:T(8,128)(2,1)}, u32[]{:S(2)}, u32[]{:S(2)}) collective-permute-start(bf16[2,256,512]{2,1,0:T(8,128)(2,1)} %collective-permute-done.57.refs_3_.refs_5_.refs_4_), channel_id=1, source_target_pairs={{0,4},{4,0},{8,12},{12,8},{16,20},{20,16},{24,28},{28,24},{1,5},{5... | collective-permute-start | bytes 1572872 | tf_op jit(solution)/shard_map/ppermute | solution.py:628
  33.8 20.6 %collective-permute-start.51 = (bf16[2,256,512]{2,1,0:T(8,128)(2,1)S(1)}, bf16[2,256,512]{2,1,0:T(8,128)(2,1)S(1)}, u32[]{:S(2)}, u32[]{:S(2)}) collective-permute-start(bf16[2,256,512]{2,1,0:T(8,128)(2,1)S(1)} %get-tuple-element.369.refs_0_), channel_id=1, source_target_pairs={{0,8},{4,12},{8,0},{12,4},{16,24},{20,28},{24,16},{28,20},{1,9},{5... | collective-permute-start | bytes 1572872 | tf_op jit(solution)/shard_map/ppermute | solution.py:657
  41.2 21.6 %collective-permute-start.59 = (bf16[2,256,512]{2,1,0:T(8,128)(2,1)S(1)}, bf16[2,256,512]{2,1,0:T(8,128)(2,1)}, u32[]{:S(2)}, u32[]{:S(2)}) collective-permute-start(bf16[2,256,512]{2,1,0:T(8,128)(2,1)S(1)} %get-tuple-element.375), channel_id=1, source_target_pairs={{0,16},{4,20},{8,24},{12,28},{16,0},{20,4},{24,8},{28,12},{1,17},{... | collective-permute-start | bytes 1572872 | tf_op jit(solution)/shard_map/ppermute | solution.py:658
  43.8 18.9 %collective-permute-start.60 = (bf16[2,256,512]{2,1,0:T(8,128)(2,1)S(1)}, bf16[2,256,512]{2,1,0:T(8,128)(2,1)}, u32[]{:S(2)}, u32[]{:S(2)}) collective-permute-start(bf16[2,256,512]{2,1,0:T(8,128)(2,1)S(1)} %get-tuple-element.376), channel_id=1, source_target_pairs={{0,8},{4,12},{8,0},{12,4},{16,24},{20,28},{24,16},{28,20},{1,9},{5... | collective-permute-start | bytes 1572872 | tf_op jit(solution)/shard_map/ppermute | solution.py:657
  65.5 23.9 %collective-permute-start.74 = (bf16[2,256,512]{2,1,0:T(8,128)(2,1)S(1)}, bf16[2,256,512]{2,1,0:T(8,128)(2,1)}, u32[]{:S(2)}, u32[]{:S(2)}) collective-permute-start(bf16[2,256,512]{2,1,0:T(8,128)(2,1)S(1)} %copy-done.3), channel_id=1, source_target_pairs={{0,8},{4,12},{8,0},{12,4},{16,24},{20,28},{24,16},{28,20},{1,9},{5... | collective-permute-start | bytes 1572872 | tf_op jit(solution)/shard_map/ppermute | solution.py:657
  66.6 40.4 %collective-permute-start.63 = (bf16[2,256,512]{2,1,0:T(8,128)(2,1)S(1)}, bf16[2,256,512]{2,1,0:T(8,128)(2,1)}, u32[]{:S(2)}, u32[]{:S(2)}) collective-permute-start(bf16[2,256,512]{2,1,0:T(8,128)(2,1)S(1)} %get-tuple-element.378), channel_id=1, source_target_pairs={{0,16},{4,20},{8,24},{12,28},{16,0},{20,4},{24,8},{28,12},{1,17},{... | collective-permute-start | bytes 1572872 | tf_op jit(solution)/shard_map/ppermute | solution.py:658
  67.8 36.7 %collective-permute-start.73 = (bf16[2,256,512]{2,1,0:T(8,128)(2,1)S(1)}, bf16[2,256,512]{2,1,0:T(8,128)(2,1)}, u32[]{:S(2)}, u32[]{:S(2)}) collective-permute-start(bf16[2,256,512]{2,1,0:T(8,128)(2,1)S(1)} %get-tuple-element.383), channel_id=1, source_target_pairs={{0,16},{4,20},{8,24},{12,28},{16,0},{20,4},{24,8},{28,12},{1,17},{... | collective-permute-start | bytes 1572872 | tf_op jit(solution)/shard_map/ppermute | solution.py:658
  68.6 38.8 %collective-permute-start.65 = (bf16[2,256,512]{2,1,0:T(8,128)(2,1)}, bf16[2,256,512]{2,1,0:T(8,128)(2,1)}, u32[]{:S(2)}, u32[]{:S(2)}) collective-permute-start(bf16[2,256,512]{2,1,0:T(8,128)(2,1)} %collective-permute-done.60.refs_8_.refs_10_.refs_4_), channel_id=1, source_target_pairs={{0,4},{4,0},{8,12},{12,8},{16,20},{20,16},{24,28},{28,24},{1,5},{5... | collective-permute-start | bytes 1572872 | tf_op jit(solution)/shard_map/ppermute | solution.py:628
  79.4 25.3 %collective-permute-start.71 = (bf16[2,256,512]{2,1,0:T(8,128)(2,1)}, bf16[2,256,512]{2,1,0:T(8,128)(2,1)}, u32[]{:S(2)}, u32[]{:S(2)}) collective-permute-start(bf16[2,256,512]{2,1,0:T(8,128)(2,1)} %copy-done.14), channel_id=1, source_target_pairs={{0,4},{4,0},{8,12},{12,8},{16,20},{20,16},{24,28},{28,24},{1,5},{5... | collective-permute-start | bytes 1572872 | tf_op jit(solution)/shard_map/ppermute | solution.py:628
  99.6 35.6 %all-to-all-start = ((f32[32,4,2048]{2,0,1:T(8,128)}), f32[32,4,2048]{2,0,1:T(8,128)}, u32[]{:S(2)}, u32[]{:S(2)}) async-start(f32[32,4,2048]{2,0,1:T(8,128)} %bitcast.27), calls=%async_computation | async-start | bytes 2097152 | tf_op jit(solution)/shard_map/all_to_all | solution.py:688
  108.7 60.3 %collective-permute-start.93 = (bf16[8,256,512]{2,1,0:T(8,128)(2,1)}, bf16[8,256,512]{2,1,0:T(8,128)(2,1)}, u32[]{:S(2)}, u32[]{:S(2)}) collective-permute-start(bf16[8,256,512]{2,1,0:T(8,128)(2,1)} %shard_map.123.refs_0_.refs_1_.refs_3_.refs_2_), channel_id=1, source_target_pairs={{0,4},{4,0},{8,12},{12,8},{16,20},{20,16},{24,28},{28,24},{1,5},{5... | collective-permute-start | bytes 6291464 | tf_op jit(solution)/shard_map/ppermute | solution.py:628
  110.5 59.1 %collective-permute-start.94 = (bf16[8,256,512]{2,1,0:T(8,128)(2,1)}, bf16[8,256,512]{2,1,0:T(8,128)(2,1)}, u32[]{:S(2)}, u32[]{:S(2)}) collective-permute-start(bf16[8,256,512]{2,1,0:T(8,128)(2,1)} %shard_map.126.refs_0_.refs_1_.refs_3_.refs_6_), channel_id=1, source_target_pairs={{0,4},{4,0},{8,12},{12,8},{16,20},{20,16},{24,28},{28,24},{1,5},{5... | collective-permute-start | bytes 6291464 | tf_op jit(solution)/shard_map/ppermute | solution.py:628
  111.1 21.4 %collective-permute-start.68 = (bf16[2,256,512]{2,1,0:T(8,128)(2,1)S(1)}, bf16[2,256,512]{2,1,0:T(8,128)(2,1)}, u32[]{:S(2)}, u32[]{:S(2)}) collective-permute-start(bf16[2,256,512]{2,1,0:T(8,128)(2,1)S(1)} %get-tuple-element.380.refs_24_), channel_id=1, source_target_pairs={{0,8},{4,12},{8,0},{12,4},{16,24},{20,28},{24,16},{28,20},{1,9},{5... | collective-permute-start | bytes 1572872 | tf_op jit(solution)/shard_map/ppermute | solution.py:657
  149.0 20.6 %collective-permute-start.89 = (bf16[2,256,512]{2,1,0:T(8,128)(2,1)}, bf16[2,256,512]{2,1,0:T(8,128)(2,1)}, u32[]{:S(2)}, u32[]{:S(2)}) collective-permute-start(bf16[2,256,512]{2,1,0:T(8,128)(2,1)} %collective-permute-done.68.refs_12_.refs_2_), channel_id=1, source_target_pairs={{0,4},{4,0},{8,12},{12,8},{16,20},{20,16},{24,28},{28,24},{1,5},{5... | collective-permute-start | bytes 1572872 | tf_op jit(solution)/shard_map/ppermute | solution.py:628
  153.1 16.6 %collective-permute-start.90 = (bf16[2,256,512]{2,1,0:T(8,128)(2,1)}, bf16[2,256,512]{2,1,0:T(8,128)(2,1)}, u32[]{:S(2)}, u32[]{:S(2)}) collective-permute-start(bf16[2,256,512]{2,1,0:T(8,128)(2,1)} %collective-permute-done.67.refs_8_.refs_3_), channel_id=1, source_target_pairs={{0,4},{4,0},{8,12},{12,8},{16,20},{20,16},{24,28},{28,24},{1,5},{5... | collective-permute-start | bytes 1572872 | tf_op jit(solution)/shard_map/ppermute | solution.py:628
  169.6 17.4 %collective-permute-start.83 = (bf16[2,256,512]{2,1,0:T(8,128)(2,1)S(1)}, bf16[2,256,512]{2,1,0:T(8,128)(2,1)}, u32[]{:S(2)}, u32[]{:S(2)}) collective-permute-start(bf16[2,256,512]{2,1,0:T(8,128)(2,1)S(1)} %get-tuple-element.388.refs_16_), channel_id=1, source_target_pairs={{0,8},{4,12},{8,0},{12,4},{16,24},{20,28},{24,16},{28,20},{1,9},{5... | collective-permute-start | bytes 1572872 | tf_op jit(solution)/shard_map/ppermute | solution.py:657
  169.7 23.2 %collective-permute-start.84 = (bf16[2,256,512]{2,1,0:T(8,128)(2,1)S(1)}, bf16[2,256,512]{2,1,0:T(8,128)(2,1)}, u32[]{:S(2)}, u32[]{:S(2)}) collective-permute-start(bf16[2,256,512]{2,1,0:T(8,128)(2,1)S(1)} %get-tuple-element.389), channel_id=1, source_target_pairs={{0,16},{4,20},{8,24},{12,28},{16,0},{20,4},{24,8},{28,12},{1,17},{... | collective-permute-start | bytes 1572872 | tf_op jit(solution)/shard_map/ppermute | solution.py:658
  176.4 29.3 %collective-permute-start.92 = (bf16[2,256,512]{2,1,0:T(8,128)(2,1)}, bf16[2,256,512]{2,1,0:T(8,128)(2,1)}, u32[]{:S(2)}, u32[]{:S(2)}) collective-permute-start(bf16[2,256,512]{2,1,0:T(8,128)(2,1)} %copy-done.21), channel_id=1, source_target_pairs={{0,4},{4,0},{8,12},{12,8},{16,20},{20,16},{24,28},{28,24},{1,5},{5... | collective-permute-start | bytes 1572872 | tf_op jit(solution)/shard_map/ppermute | solution.py:628
  184.0 26.0 %collective-permute-start.85 = (bf16[2,256,512]{2,1,0:T(8,128)(2,1)}, bf16[2,256,512]{2,1,0:T(8,128)(2,1)}, u32[]{:S(2)}, u32[]{:S(2)}) collective-permute-start(bf16[2,256,512]{2,1,0:T(8,128)(2,1)} %collective-permute-done.69), channel_id=1, source_target_pairs={{0,4},{4,0},{8,12},{12,8},{16,20},{20,16},{24,28},{28,24},{1,5},{5... | collective-permute-start | bytes 1572872 | tf_op jit(solution)/shard_map/ppermute | solution.py:628
  184.0 26.0 %collective-permute-start.86 = (bf16[2,256,512]{2,1,0:T(8,128)(2,1)}, bf16[2,256,512]{2,1,0:T(8,128)(2,1)}, u32[]{:S(2)}, u32[]{:S(2)}) collective-permute-start(bf16[2,256,512]{2,1,0:T(8,128)(2,1)} %collective-permute-done.70), channel_id=1, source_target_pairs={{0,4},{4,0},{8,12},{12,8},{16,20},{20,16},{24,28},{28,24},{1,5},{5... | collective-permute-start | bytes 1572872 | tf_op jit(solution)/shard_map/ppermute | solution.py:628
  187.0 23.0 %collective-permute-start.87 = (bf16[2,256,512]{2,1,0:T(8,128)(2,1)}, bf16[2,256,512]{2,1,0:T(8,128)(2,1)}, u32[]{:S(2)}, u32[]{:S(2)}) collective-permute-start(bf16[2,256,512]{2,1,0:T(8,128)(2,1)} %collective-permute-done.83), channel_id=1, source_target_pairs={{0,4},{4,0},{8,12},{12,8},{16,20},{20,16},{24,28},{28,24},{1,5},{5... | collective-permute-start | bytes 1572872 | tf_op jit(solution)/shard_map/ppermute | solution.py:628
  192.9 17.1 %collective-permute-start.88 = (bf16[2,256,512]{2,1,0:T(8,128)(2,1)}, bf16[2,256,512]{2,1,0:T(8,128)(2,1)}, u32[]{:S(2)}, u32[]{:S(2)}) collective-permute-start(bf16[2,256,512]{2,1,0:T(8,128)(2,1)} %collective-permute-done.84), channel_id=1, source_target_pairs={{0,4},{4,0},{8,12},{12,8},{16,20},{20,16},{24,28},{28,24},{1,5},{5... | collective-permute-start | bytes 1572872 | tf_op jit(solution)/shard_map/ppermute | solution.py:628
  (48 other events, 511.1 us)

commit v3 on v2

--- a/solution.py
+++ b/solution.py
@@ -479,9 +479,9 @@
 
 def add_kernel(parts_ref, residual_ref, stream_ref, squares_ref):
     total = residual_ref[0].astype(jnp.float32)
-    added = parts_ref[0]
+    added = parts_ref[0].astype(jnp.float32)
     for part in range(1, parts_ref.shape[0]):
-        added = added + parts_ref[part]
+        added = added + parts_ref[part].astype(jnp.float32)
     total = total + added
     stream_ref[...] = total
     squares = jnp.sum(total * total, axis=-1, keepdims=True)
@@ -497,7 +497,7 @@
             jax.ShapeDtypeStruct((rows, 128), jnp.float32),
         ),
         cost_estimate=pl.CostEstimate(
-            flops=8 * parts.size, bytes_accessed=4 * parts.size, transcendentals=0
+            flops=8 * parts.size, bytes_accessed=2 * parts.size, transcendentals=0
         ),
     )(parts, residual)
 
@@ -682,6 +682,8 @@
             preferred_element_type=jnp.float32,
         )
         work.partial = product if head == 0 else work.partial + product
+        if head == kv_heads - 1:
+            work.partial = work.partial.astype(jnp.bfloat16)
         return [work.partial]
 
     def add_parts():

time: 212 us -> 210 us (level)
  waiting for transfers between devices: 82.8 us -> 79.4 us
    ppermute x10, waiting for transfers between devices: 52.9 us -> 29.1 us  [send(): landed_x = lax.ppermute(out_x, SECTION, across_x)]
    ppermute x10, waiting for transfers between devices: 22.9 us -> 36.4 us  [send(): landed_y = lax.ppermute(out_y, SECTION, across_y)]
    all_to_all x1, waiting for transfers between devices: 0.01 us -> 8.55 us  [add_parts(): lax.all_to_all(work.partial, TENSOR, split_axis=1, concat_axis=0, tiled=T...]
    ppermute x10, starting transfers between devices: 10.7 us -> 13.1 us  [send(): landed_y = lax.ppermute(out_y, SECTION, across_y)]
    unnamed x45 -> x43, local copies, waits for them, and re-layouts: 3.05 us -> 4.67 us
  transfers between devices with their start and end apart: 50 -> 50, of which waited for: 17 -> 17; matrix products, arithmetic and copies ran while one was open for 11% -> 11% of each run, Pallas kernels for 23% -> 24%
where the time goes in v3:
time: 210 us; the launch traced here: 209 us
  waiting for transfers between devices  79.4 us (38%)
  Pallas kernels  58.5 us (28%)
  starting transfers between devices  43 us (20%)
  matrix products  18.8 us (9%)
  local copies, waits for them, and re-layouts  7.35 us (4%)
    ppermute x10, waiting for transfers between devices, send(): landed_y = lax.ppermute(out_y, SECTION, across_y)  36.4 us
    ppermute x10, waiting for transfers between devices, send(): landed_x = lax.ppermute(out_x, SECTION, across_x)  29.1 us
    dot_general x2, matrix products, project_head(): jnp.dot(work.attended.reshape(rows, -1), out_weight[0, head * depth:(head...  18.8 us
    pallas_call x10, Pallas kernels, pick_pieces(): pl.pallas_call(functools.partial(pick_kernel, step, len(near), len(after)...  17.6 us
    ppermute x10, starting transfers between devices, send(): landed_y = lax.ppermute(out_y, SECTION, across_y)  13.1 us
    pallas_call x4, Pallas kernels, write_tokens(): pl.pallas_call(functools.partial(write_kernel, rows, first_of), out_shape...  12.9 us
    pallas_call x2, Pallas kernels, attend(): pl.pallas_call(functools.partial(attend_kernel, block), out_shape=jax.Sha...  11 us
    ppermute x10, starting transfers between devices, send(): landed_x = lax.ppermute(out_x, SECTION, across_x)  10.7 us
  transfers between devices with their start and end apart: 50, of which 17 were waited for; matrix products, arithmetic and copies ran while one was open for 11% of the time, Pallas kernels for 24%

profile of v3, /device:TPU:0, one launch (start us, length us, event | category | flops | bytes accessed | tf_op | source)
XLA Modules:
  0.0 209.0 jit_solution(16783461382047235545)
XLA Ops:
  0.6 3.3 %shard_map.122.refs_0_.refs_12_ = bf16[8,256,512]{2,1,0:T(8,128)(2,1)} custom-call(s32[1]{0:T(128)} %bitcast.place_ref, s32[32]{0:T(128)} %lengths_ref.11, bf16[1,32,256,512]{3,2,1,0:T(8,128)(2,1)} %cache_ref.11, bf16[1,32,512]{2,1,0:T(8,128)(2,1)} %fresh_ref.11), custom_call_target="tpu_custom_call" | custom-call | flops 2097152 | bytes 4194304 | tf_op jit(solution)/shard_map/pallas_call | solution.py:249
  6.9 3.2 %shard_map.123.refs_0_.refs_1_.refs_3_.refs_2_ = bf16[8,256,512]{2,1,0:T(8,128)(2,1)} custom-call(s32[1]{0:T(128)} %bitcast.place_ref, s32[32]{0:T(128)} %lengths_ref.11, bf16[1,32,256,512]{3,2,1,0:T(8,128)(2,1)} %cache_ref.11, bf16[1,32,512]{2,1,0:T(8,128)(2,1)} %fresh_ref.11, bf16[8,256,512]{2,1,0:T(8,128)(2,1)} %shard_map.122.refs_0_.refs_12_), custom_call_target="tpu_custom_call" | custom-call | flops 2097152 | bytes 4194304 | tf_op jit(solution)/shard_map/pallas_call | solution.py:249
  12.6 3.2 %shard_map.125.refs_0_.refs_18_ = bf16[8,256,512]{2,1,0:T(8,128)(2,1)} custom-call(s32[1]{0:T(128)} %bitcast.place_ref, s32[32]{0:T(128)} %lengths_ref.11, bf16[1,32,256,512]{3,2,1,0:T(8,128)(2,1)} %cache_ref.11, bf16[1,32,512]{2,1,0:T(8,128)(2,1)} %fresh_ref.11, bf16[2,256,512]{2,1,0:T(8,128)(2,1)} %copy-done.4), custom_call_target="tpu_custom_call" | custom-call | flops 2097152 | bytes 4194304 | tf_op jit(solution)/shard_map/pallas_call | solution.py:249
  16.0 3.0 %collective-permute-start.55 = (bf16[2,256,512]{2,1,0:T(8,128)(2,1)S(1)}, bf16[2,256,512]{2,1,0:T(8,128)(2,1)}, u32[]{:S(2)}, u32[]{:S(2)}) collective-permute-start(bf16[2,256,512]{2,1,0:T(8,128)(2,1)S(1)} %copy-done.5), channel_id=1, source_target_pairs={{0,8},{4,12},{8,0},{12,4},{16,24},{20,28},{24,16},{28,20},{1,9},{5... | collective-permute-start | bytes 1572872 | tf_op jit(solution)/shard_map/ppermute | solution.py:657
  20.5 3.2 %shard_map.126.refs_0_.refs_1_.refs_3_.refs_6_ = bf16[8,256,512]{2,1,0:T(8,128)(2,1)} custom-call(s32[1]{0:T(128)} %bitcast.place_ref, s32[32]{0:T(128)} %lengths_ref.11, bf16[1,32,256,512]{3,2,1,0:T(8,128)(2,1)} %cache_ref.11, bf16[1,32,512]{2,1,0:T(8,128)(2,1)} %fresh_ref.11, bf16[8,256,512]{2,1,0:T(8,128)(2,1)} %shard_map.125.refs_0_.refs_18_), custom_call_target="tpu_custom_call" | custom-call | flops 2097152 | bytes 4194304 | tf_op jit(solution)/shard_map/pallas_call | solution.py:249
  26.7 4.5 %collective-permute-done.55.refs_4_.refs_7_.refs_9_.refs_2_ = bf16[2,256,512]{2,1,0:T(8,128)(2,1)} collective-permute-done((bf16[2,256,512]{2,1,0:T(8,128)(2,1)S(1)}, bf16[2,256,512]{2,1,0:T(8,128)(2,1)}, u32[]{:S(2)}, u32[]{:S(2)}) %collective-permute-start.55) | collective-permute-done | bytes 524320 | tf_op jit(solution)/shard_map/ppermute | solution.py:657
  33.9 5.5 %shard_map.128.refs_0_ = bf16[32,8,128]{2,1,0:T(8,128)(2,1)} custom-call(s32[32]{0:T(128)} %lengths_ref.11, bf16[32,16,128]{2,1,0:T(8,128)(2,1)} %bitcast.30, bf16[1,32,256,512]{3,2,1,0:T(8,128)(2,1)} %cache_ref.11, bf16[1,32,512]{2,1,0:T(8,128)(2,1)} %fresh_ref.11, bf16[2,256,512]{2,1,0:T(8,128)(2,1)} %copy-done.3), custom_call_target="tpu_custom_call" | custom-call | flops 251658240 | bytes 4194304 | tf_op jit(solution)/shard_map/pallas_call | solution.py:460
  44.7 9.8 %fusion.2.refs_0_ = f32[32,8192]{1,0:T(8,128)} fusion(bf16[1,2048,8192]{2,1,0:T(8,128)(2,1)} %param.20, bf16[4,8,8,128]{3,2,1,0:T(8,128)(2,1)} %bitcast.33), kind=kOutput, calls=%fused_computation.3 | convolution fusion | flops 536870912 | bytes 17891328 | tf_op jit(solution)/shard_map/dot_general | solution.py:679
  57.3 5.5 %shard_map.130.refs_0_ = bf16[32,8,128]{2,1,0:T(8,128)(2,1)} custom-call(s32[32]{0:T(128)} %lengths_ref.11, bf16[32,16,128]{2,1,0:T(8,128)(2,1)} %bitcast.31, bf16[1,32,256,512]{3,2,1,0:T(8,128)(2,1)} %cache_ref.11, bf16[1,32,512]{2,1,0:T(8,128)(2,1)} %fresh_ref.11, bf16[2,256,512]{2,1,0:T(8,128)(2,1)} %copy-done.2), custom_call_target="tpu_custom_call" | custom-call | flops 251658240 | bytes 4194304 | tf_op jit(solution)/shard_map/pallas_call | solution.py:460
  67.8 9.0 %fusion.9.refs_0_ = bf16[32,8192]{1,0:T(8,128)(2,1)S(1)} fusion(f32[32,8192]{1,0:T(8,128)} %fusion.2.refs_0_, bf16[1,2048,8192]{2,1,0:T(8,128)(2,1)} %param.20, bf16[4,8,8,128]{3,2,1,0:T(8,128)(2,1)} %bitcast.32), kind=kOutput, calls=%fused_computation.8 | convolution fusion | flops 537395200 | bytes 18415616 | tf_op jit(solution)/shard_map/dot_general | solution.py:679
  78.4 4.9 %all-to-all-start = ((bf16[32,4,2048]{2,0,1:T(8,128)(2,1)}), bf16[32,4,2048]{2,0,1:T(8,128)(2,1)}, u32[]{:S(2)}, u32[]{:S(2)}) async-start(bf16[32,4,2048]{2,0,1:T(8,128)(2,1)} %bitcast.29), calls=%async_computation | async-start | bytes 1048576 | tf_op jit(solution)/shard_map/all_to_all | solution.py:690
  84.3 5.7 %collective-permute-done.73.refs_6_.refs_11_ = bf16[2,256,512]{2,1,0:T(8,128)(2,1)} collective-permute-done((bf16[2,256,512]{2,1,0:T(8,128)(2,1)S(1)}, bf16[2,256,512]{2,1,0:T(8,128)(2,1)}, u32[]{:S(2)}, u32[]{:S(2)}) %collective-permute-start.73) | collective-permute-done | bytes 524320 | tf_op jit(solution)/shard_map/ppermute | solution.py:658
  90.0 8.5 %all-to-all-done = bf16[32,4,2048]{2,0,1:T(8,128)(2,1)} async-done(((bf16[32,4,2048]{2,0,1:T(8,128)(2,1)}), bf16[32,4,2048]{2,0,1:T(8,128)(2,1)}, u32[]{:S(2)}, u32[]{:S(2)}) %all-to-all-start) | async-done | bytes 524320 | tf_op jit(solution)/shard_map/all_to_all | solution.py:690
  112.5 9.4 %collective-permute-done.75.refs_10_.refs_11_.refs_4_ = bf16[2,256,512]{2,1,0:T(8,128)(2,1)} collective-permute-done((bf16[2,256,512]{2,1,0:T(8,128)(2,1)S(1)}, bf16[2,256,512]{2,1,0:T(8,128)(2,1)}, u32[]{:S(2)}, u32[]{:S(2)}) %collective-permute-start.75) | collective-permute-done | bytes 524320 | tf_op jit(solution)/shard_map/ppermute | solution.py:657
  124.7 6.1 %collective-permute-done.68.refs_12_.refs_2_ = bf16[2,256,512]{2,1,0:T(8,128)(2,1)S(1)} collective-permute-done((bf16[2,256,512]{2,1,0:T(8,128)(2,1)S(1)}, bf16[2,256,512]{2,1,0:T(8,128)(2,1)S(1)}, u32[]{:S(2)}, u32[]{:S(2)}) %collective-permute-start.68) | collective-permute-done | bytes 524320 | tf_op jit(solution)/shard_map/ppermute | solution.py:657
  137.9 10.5 %collective-permute-done.81.refs_8_.refs_7_ = bf16[2,256,512]{2,1,0:T(8,128)(2,1)S(1)} collective-permute-done((bf16[2,256,512]{2,1,0:T(8,128)(2,1)S(1)}, bf16[2,256,512]{2,1,0:T(8,128)(2,1)S(1)}, u32[]{:S(2)}, u32[]{:S(2)}) %collective-permute-start.81) | collective-permute-done | bytes 524320 | tf_op jit(solution)/shard_map/ppermute | solution.py:658
  153.0 3.4 %all-to-all-start.1 = ((bf16[8,8,2048]{2,1,0:T(8,128)(2,1)}), bf16[8,8,2048]{2,1,0:T(8,128)(2,1)S(1)}, u32[]{:S(2)}, u32[]{:S(2)}) async-start(bf16[8,8,2048]{2,1,0:T(8,128)(2,1)} %shard_map.132.refs_0_), calls=%async_computation.1 | async-start | bytes 524288 | tf_op jit(solution)/shard_map/all_to_all | solution.py:707
  160.2 3.6 %all-to-all-done.1 = bf16[8,8,2048]{2,1,0:T(8,128)(2,1)S(1)} async-done(((bf16[8,8,2048]{2,1,0:T(8,128)(2,1)}), bf16[8,8,2048]{2,1,0:T(8,128)(2,1)S(1)}, u32[]{:S(2)}, u32[]{:S(2)}) %all-to-all-start.1) | async-done | bytes 262176 | tf_op jit(solution)/shard_map/all_to_all | solution.py:707
  169.2 5.1 %collective-permute-done.69 = bf16[2,256,512]{2,1,0:T(8,128)(2,1)} collective-permute-done((bf16[2,256,512]{2,1,0:T(8,128)(2,1)S(1)}, bf16[2,256,512]{2,1,0:T(8,128)(2,1)}, u32[]{:S(2)}, u32[]{:S(2)}) %collective-permute-start.69) | collective-permute-done | bytes 524320 | tf_op jit(solution)/shard_map/ppermute | solution.py:657
  174.3 7.6 %collective-permute-done.70 = bf16[2,256,512]{2,1,0:T(8,128)(2,1)} collective-permute-done((bf16[2,256,512]{2,1,0:T(8,128)(2,1)S(1)}, bf16[2,256,512]{2,1,0:T(8,128)(2,1)}, u32[]{:S(2)}, u32[]{:S(2)}) %collective-permute-start.70) | collective-permute-done | bytes 524320 | tf_op jit(solution)/shard_map/ppermute | solution.py:658
  184.9 5.9 %collective-permute-done.84 = bf16[2,256,512]{2,1,0:T(8,128)(2,1)} collective-permute-done((bf16[2,256,512]{2,1,0:T(8,128)(2,1)S(1)}, bf16[2,256,512]{2,1,0:T(8,128)(2,1)}, u32[]{:S(2)}, u32[]{:S(2)}) %collective-permute-start.84) | collective-permute-done | bytes 524320 | tf_op jit(solution)/shard_map/ppermute | solution.py:658
  190.9 3.4 %all-to-all-start.2 = ((bf16[8,8,2048]{2,1,0:T(8,128)(2,1)}), bf16[8,8,2048]{2,1,0:T(8,128)(2,1)S(1)}, u32[]{:S(2)}, u32[]{:S(2)}) async-start(bf16[8,8,2048]{2,1,0:T(8,128)(2,1)} %gather_fusion), calls=%async_computation.2 | async-start | bytes 524288 | tf_op jit(solution)/shard_map/all_to_all | solution.py:709
  195.5 3.9 %shard_map.140.refs_17_ = bf16[1,32,256,512]{3,2,1,0:T(8,128)(2,1)} custom-call(s32[1]{0:T(128)} %bitcast.place_ref, s32[32]{0:T(128)S(1)} %shard_map.121.ids_ref, bf16[8,256,512]{2,1,0:T(8,128)(2,1)} %shard_map.123.refs_0_.refs_1_.refs_3_.refs_2_, bf16[8,256,512]{2,1,0:T(8,128)(2,1)} %collective-permute-done.48.refs_1_.refs_2_.refs_4_.refs_3_, ...), custom_call_target="tpu_custom_call" | custom-call | flops 4194304 | bytes 8388608 | tf_op jit(solution)/shard_map/pallas_call | solution.py:399
  203.5 4.3 %shard_map.141 = bf16[1,32,256,512]{3,2,1,0:T(8,128)(2,1)} custom-call(s32[1]{0:T(128)} %bitcast.place_ref, s32[32]{0:T(128)S(1)} %shard_map.121.ids_ref, bf16[2,256,512]{2,1,0:T(8,128)(2,1)} %collective-permute-done.61.refs_9_.refs_11_.refs_0_, ...), custom_call_target="tpu_custom_call", output_to_operand_aliasing={{}: (19, {})} | custom-call | flops 4194304 | bytes 8388608 | tf_op jit(solution)/shard_map/pallas_call | solution.py:399
  (149 shorter events, 75.4 us)
Async XLA Ops:
  25.5 18.3 %collective-permute-start.50 = (bf16[2,256,512]{2,1,0:T(8,128)(2,1)S(1)}, bf16[2,256,512]{2,1,0:T(8,128)(2,1)S(1)}, u32[]{:S(2)}, u32[]{:S(2)}) collective-permute-start(bf16[2,256,512]{2,1,0:T(8,128)(2,1)S(1)} %get-tuple-element.370), channel_id=1, source_target_pairs={{0,16},{4,20},{8,24},{12,28},{16,0},{20,4},{24,8},{28,12},{1,17},{... | collective-permute-start | bytes 1572872 | tf_op jit(solution)/shard_map/ppermute | solution.py:658
  31.2 31.6 %collective-permute-start.56 = (bf16[2,256,512]{2,1,0:T(8,128)(2,1)}, bf16[2,256,512]{2,1,0:T(8,128)(2,1)}, u32[]{:S(2)}, u32[]{:S(2)}) collective-permute-start(bf16[2,256,512]{2,1,0:T(8,128)(2,1)} %collective-permute-done.55.refs_4_.refs_7_.refs_9_.refs_2_), channel_id=1, source_target_pairs={{0,4},{4,0},{8,12},{12,8},{16,20},{20,16},{24,28},{28,24},{1,5},{5... | collective-permute-start | bytes 1572872 | tf_op jit(solution)/shard_map/ppermute | solution.py:628
  33.8 28.9 %collective-permute-start.58 = (bf16[2,256,512]{2,1,0:T(8,128)(2,1)}, bf16[2,256,512]{2,1,0:T(8,128)(2,1)}, u32[]{:S(2)}, u32[]{:S(2)}) collective-permute-start(bf16[2,256,512]{2,1,0:T(8,128)(2,1)} %collective-permute-done.57.refs_3_.refs_5_.refs_4_), channel_id=1, source_target_pairs={{0,4},{4,0},{8,12},{12,8},{16,20},{20,16},{24,28},{28,24},{1,5},{5... | collective-permute-start | bytes 1572872 | tf_op jit(solution)/shard_map/ppermute | solution.py:628
  33.8 20.6 %collective-permute-start.51 = (bf16[2,256,512]{2,1,0:T(8,128)(2,1)S(1)}, bf16[2,256,512]{2,1,0:T(8,128)(2,1)S(1)}, u32[]{:S(2)}, u32[]{:S(2)}) collective-permute-start(bf16[2,256,512]{2,1,0:T(8,128)(2,1)S(1)} %get-tuple-element.369.refs_0_), channel_id=1, source_target_pairs={{0,8},{4,12},{8,0},{12,4},{16,24},{20,28},{24,16},{28,20},{1,9},{5... | collective-permute-start | bytes 1572872 | tf_op jit(solution)/shard_map/ppermute | solution.py:657
  41.2 21.6 %collective-permute-start.59 = (bf16[2,256,512]{2,1,0:T(8,128)(2,1)S(1)}, bf16[2,256,512]{2,1,0:T(8,128)(2,1)}, u32[]{:S(2)}, u32[]{:S(2)}) collective-permute-start(bf16[2,256,512]{2,1,0:T(8,128)(2,1)S(1)} %get-tuple-element.375), channel_id=1, source_target_pairs={{0,16},{4,20},{8,24},{12,28},{16,0},{20,4},{24,8},{28,12},{1,17},{... | collective-permute-start | bytes 1572872 | tf_op jit(solution)/shard_map/ppermute | solution.py:658
  43.8 19.0 %collective-permute-start.60 = (bf16[2,256,512]{2,1,0:T(8,128)(2,1)S(1)}, bf16[2,256,512]{2,1,0:T(8,128)(2,1)}, u32[]{:S(2)}, u32[]{:S(2)}) collective-permute-start(bf16[2,256,512]{2,1,0:T(8,128)(2,1)S(1)} %get-tuple-element.376), channel_id=1, source_target_pairs={{0,8},{4,12},{8,0},{12,4},{16,24},{20,28},{24,16},{28,20},{1,9},{5... | collective-permute-start | bytes 1572872 | tf_op jit(solution)/shard_map/ppermute | solution.py:657
  56.3 27.8 %collective-permute-start.74 = (bf16[2,256,512]{2,1,0:T(8,128)(2,1)S(1)}, bf16[2,256,512]{2,1,0:T(8,128)(2,1)}, u32[]{:S(2)}, u32[]{:S(2)}) collective-permute-start(bf16[2,256,512]{2,1,0:T(8,128)(2,1)S(1)} %get-tuple-element.371.refs_0_), channel_id=1, source_target_pairs={{0,8},{4,12},{8,0},{12,4},{16,24},{20,28},{24,16},{28,20},{1,9},{5... | collective-permute-start | bytes 1572872 | tf_op jit(solution)/shard_map/ppermute | solution.py:657
  64.6 18.7 %collective-permute-start.61 = (bf16[2,256,512]{2,1,0:T(8,128)(2,1)S(1)}, bf16[2,256,512]{2,1,0:T(8,128)(2,1)}, u32[]{:S(2)}, u32[]{:S(2)}) collective-permute-start(bf16[2,256,512]{2,1,0:T(8,128)(2,1)S(1)} %get-tuple-element.377), channel_id=1, source_target_pairs={{0,8},{4,12},{8,0},{12,4},{16,24},{20,28},{24,16},{28,20},{1,9},{5... | collective-permute-start | bytes 1572872 | tf_op jit(solution)/shard_map/ppermute | solution.py:657
  65.7 17.8 %collective-permute-start.63 = (bf16[2,256,512]{2,1,0:T(8,128)(2,1)S(1)}, bf16[2,256,512]{2,1,0:T(8,128)(2,1)}, u32[]{:S(2)}, u32[]{:S(2)}) collective-permute-start(bf16[2,256,512]{2,1,0:T(8,128)(2,1)S(1)} %get-tuple-element.378), channel_id=1, source_target_pairs={{0,16},{4,20},{8,24},{12,28},{16,0},{20,4},{24,8},{28,12},{1,17},{... | collective-permute-start | bytes 1572872 | tf_op jit(solution)/shard_map/ppermute | solution.py:658
  67.1 22.9 %collective-permute-start.73 = (bf16[2,256,512]{2,1,0:T(8,128)(2,1)S(1)}, bf16[2,256,512]{2,1,0:T(8,128)(2,1)}, u32[]{:S(2)}, u32[]{:S(2)}) collective-permute-start(bf16[2,256,512]{2,1,0:T(8,128)(2,1)S(1)} %get-tuple-element.383), channel_id=1, source_target_pairs={{0,16},{4,20},{8,24},{12,28},{16,0},{20,4},{24,8},{28,12},{1,17},{... | collective-permute-start | bytes 1572872 | tf_op jit(solution)/shard_map/ppermute | solution.py:658
  78.4 20.1 %all-to-all-start = ((bf16[32,4,2048]{2,0,1:T(8,128)(2,1)}), bf16[32,4,2048]{2,0,1:T(8,128)(2,1)}, u32[]{:S(2)}, u32[]{:S(2)}) async-start(bf16[32,4,2048]{2,0,1:T(8,128)(2,1)} %bitcast.29), calls=%async_computation | async-start | bytes 1048576 | tf_op jit(solution)/shard_map/all_to_all | solution.py:690
  83.3 17.1 %collective-permute-start.66 = (bf16[2,256,512]{2,1,0:T(8,128)(2,1)}, bf16[2,256,512]{2,1,0:T(8,128)(2,1)S(1)}, u32[]{:S(2)}, u32[]{:S(2)}) collective-permute-start(bf16[2,256,512]{2,1,0:T(8,128)(2,1)} %collective-permute-done.59.refs_6_.refs_5_), channel_id=1, source_target_pairs={{0,4},{4,0},{8,12},{12,8},{16,20},{20,16},{24,28},{28,24},{1,5},{5... | collective-permute-start | bytes 1572872 | tf_op jit(solution)/shard_map/ppermute | solution.py:628
  83.8 18.7 %collective-permute-start.72 = (bf16[2,256,512]{2,1,0:T(8,128)(2,1)S(1)}, bf16[2,256,512]{2,1,0:T(8,128)(2,1)}, u32[]{:S(2)}, u32[]{:S(2)}) collective-permute-start(bf16[2,256,512]{2,1,0:T(8,128)(2,1)S(1)} %collective-permute-done.50.refs_3_.refs_5_.refs_9_), channel_id=1, source_target_pairs={{0,4},{4,0},{8,12},{12,8},{16,20},{20,16},{24,28},{28,24},{1,5},{5... | collective-permute-start | bytes 1572872 | tf_op jit(solution)/shard_map/ppermute | solution.py:628
  84.0 27.5 %collective-permute-start.79 = (bf16[2,256,512]{2,1,0:T(8,128)(2,1)}, bf16[2,256,512]{2,1,0:T(8,128)(2,1)}, u32[]{:S(2)}, u32[]{:S(2)}) collective-permute-start(bf16[2,256,512]{2,1,0:T(8,128)(2,1)} %collective-permute-done.74.refs_8_.refs_9_.refs_10_), channel_id=1, source_target_pairs={{0,4},{4,0},{8,12},{12,8},{16,20},{20,16},{24,28},{28,24},{1,5},{5... | collective-permute-start | bytes 1572872 | tf_op jit(solution)/shard_map/ppermute | solution.py:628
  90.0 21.7 %collective-permute-start.80 = (bf16[2,256,512]{2,1,0:T(8,128)(2,1)}, bf16[2,256,512]{2,1,0:T(8,128)(2,1)}, u32[]{:S(2)}, u32[]{:S(2)}) collective-permute-start(bf16[2,256,512]{2,1,0:T(8,128)(2,1)} %collective-permute-done.73.refs_6_.refs_11_), channel_id=1, source_target_pairs={{0,4},{4,0},{8,12},{12,8},{16,20},{20,16},{24,28},{28,24},{1,5},{5... | collective-permute-start | bytes 1572872 | tf_op jit(solution)/shard_map/ppermute | solution.py:628
  109.7 57.2 %collective-permute-start.93 = (bf16[8,256,512]{2,1,0:T(8,128)(2,1)}, bf16[8,256,512]{2,1,0:T(8,128)(2,1)}, u32[]{:S(2)}, u32[]{:S(2)}) collective-permute-start(bf16[8,256,512]{2,1,0:T(8,128)(2,1)} %shard_map.123.refs_0_.refs_1_.refs_3_.refs_2_), channel_id=1, source_target_pairs={{0,4},{4,0},{8,12},{12,8},{16,20},{20,16},{24,28},{28,24},{1,5},{5... | collective-permute-start | bytes 6291464 | tf_op jit(solution)/shard_map/ppermute | solution.py:628
  111.6 55.9 %collective-permute-start.94 = (bf16[8,256,512]{2,1,0:T(8,128)(2,1)}, bf16[8,256,512]{2,1,0:T(8,128)(2,1)}, u32[]{:S(2)}, u32[]{:S(2)}) collective-permute-start(bf16[8,256,512]{2,1,0:T(8,128)(2,1)} %shard_map.126.refs_0_.refs_1_.refs_3_.refs_6_), channel_id=1, source_target_pairs={{0,4},{4,0},{8,12},{12,8},{16,20},{20,16},{24,28},{28,24},{1,5},{5... | collective-permute-start | bytes 6291464 | tf_op jit(solution)/shard_map/ppermute | solution.py:628
  111.7 19.1 %collective-permute-start.68 = (bf16[2,256,512]{2,1,0:T(8,128)(2,1)S(1)}, bf16[2,256,512]{2,1,0:T(8,128)(2,1)S(1)}, u32[]{:S(2)}, u32[]{:S(2)}) collective-permute-start(bf16[2,256,512]{2,1,0:T(8,128)(2,1)S(1)} %get-tuple-element.380.refs_24_), channel_id=1, source_target_pairs={{0,8},{4,12},{8,0},{12,4},{16,24},{20,28},{24,16},{28,20},{1,9},{5... | collective-permute-start | bytes 1572872 | tf_op jit(solution)/shard_map/ppermute | solution.py:657
  167.5 17.4 %collective-permute-start.83 = (bf16[2,256,512]{2,1,0:T(8,128)(2,1)S(1)}, bf16[2,256,512]{2,1,0:T(8,128)(2,1)}, u32[]{:S(2)}, u32[]{:S(2)}) collective-permute-start(bf16[2,256,512]{2,1,0:T(8,128)(2,1)S(1)} %get-tuple-element.388.refs_16_), channel_id=1, source_target_pairs={{0,8},{4,12},{8,0},{12,4},{16,24},{20,28},{24,16},{28,20},{1,9},{5... | collective-permute-start | bytes 1572872 | tf_op jit(solution)/shard_map/ppermute | solution.py:657
  167.6 23.2 %collective-permute-start.84 = (bf16[2,256,512]{2,1,0:T(8,128)(2,1)S(1)}, bf16[2,256,512]{2,1,0:T(8,128)(2,1)}, u32[]{:S(2)}, u32[]{:S(2)}) collective-permute-start(bf16[2,256,512]{2,1,0:T(8,128)(2,1)S(1)} %get-tuple-element.389), channel_id=1, source_target_pairs={{0,16},{4,20},{8,24},{12,28},{16,0},{20,4},{24,8},{28,12},{1,17},{... | collective-permute-start | bytes 1572872 | tf_op jit(solution)/shard_map/ppermute | solution.py:658
  174.3 29.2 %collective-permute-start.92 = (bf16[2,256,512]{2,1,0:T(8,128)(2,1)}, bf16[2,256,512]{2,1,0:T(8,128)(2,1)}, u32[]{:S(2)}, u32[]{:S(2)}) collective-permute-start(bf16[2,256,512]{2,1,0:T(8,128)(2,1)} %copy-done.19), channel_id=1, source_target_pairs={{0,4},{4,0},{8,12},{12,8},{16,20},{20,16},{24,28},{28,24},{1,5},{5... | collective-permute-start | bytes 1572872 | tf_op jit(solution)/shard_map/ppermute | solution.py:628
  181.9 26.0 %collective-permute-start.85 = (bf16[2,256,512]{2,1,0:T(8,128)(2,1)}, bf16[2,256,512]{2,1,0:T(8,128)(2,1)}, u32[]{:S(2)}, u32[]{:S(2)}) collective-permute-start(bf16[2,256,512]{2,1,0:T(8,128)(2,1)} %collective-permute-done.69), channel_id=1, source_target_pairs={{0,4},{4,0},{8,12},{12,8},{16,20},{20,16},{24,28},{28,24},{1,5},{5... | collective-permute-start | bytes 1572872 | tf_op jit(solution)/shard_map/ppermute | solution.py:628
  181.9 26.0 %collective-permute-start.86 = (bf16[2,256,512]{2,1,0:T(8,128)(2,1)}, bf16[2,256,512]{2,1,0:T(8,128)(2,1)}, u32[]{:S(2)}, u32[]{:S(2)}) collective-permute-start(bf16[2,256,512]{2,1,0:T(8,128)(2,1)} %collective-permute-done.70), channel_id=1, source_target_pairs={{0,4},{4,0},{8,12},{12,8},{16,20},{20,16},{24,28},{28,24},{1,5},{5... | collective-permute-start | bytes 1572872 | tf_op jit(solution)/shard_map/ppermute | solution.py:628
  184.9 22.9 %collective-permute-start.87 = (bf16[2,256,512]{2,1,0:T(8,128)(2,1)}, bf16[2,256,512]{2,1,0:T(8,128)(2,1)}, u32[]{:S(2)}, u32[]{:S(2)}) collective-permute-start(bf16[2,256,512]{2,1,0:T(8,128)(2,1)} %collective-permute-done.83), channel_id=1, source_target_pairs={{0,4},{4,0},{8,12},{12,8},{16,20},{20,16},{24,28},{28,24},{1,5},{5... | collective-permute-start | bytes 1572872 | tf_op jit(solution)/shard_map/ppermute | solution.py:628
  (47 other events, 631.5 us)
